TPU v7x, 64 devices: a 2x2x8 block of a 4x4x8 slice. The times are simulated.
64 devices in a mesh: data: 4 (over x, y), seq: 16 (over z, core).
Axes of the slice: x: 2, y: 2, z: 8, core: 2. Of those that a mesh axis runs over, the one named last changes fastest.
The devices are a block of a 4x4x8 slice.
Arguments:
- dec_in: bfloat16 [8192, 768], P(('data', 'seq')), parts along dimension 0
- memory: bfloat16 [65536, 768], P(('data', 'seq')), parts along dimension 0
- mem_len: int32 [4], P('data'), parts along dimension 0
- grad_out: float32 [8192, 768], P(('data', 'seq')), parts along dimension 0
- norm_attn: bfloat16 [768], replicated
- wq_cross: bfloat16 [768, 12, 64], replicated
- wk_cross: bfloat16 [768, 12, 64], replicated
- wv_cross: bfloat16 [768, 12, 64], replicated
- wo_cross: bfloat16 [12, 64, 768], replicated
- norm_mlp: bfloat16 [768], replicated
- w_gate: bfloat16 [768, 2048], replicated
- w_up: bfloat16 [768, 2048], replicated
- w_down: bfloat16 [2048, 768], replicated
Outputs:
- output 1: float32 [8192, 768], P(('data', 'seq')), parts along dimension 0
- output 2: float32 [65536, 768], P(('data', 'seq')), parts along dimension 0
- output 3: float32 [3072], P('data'), parts along dimension 0
- output 4: float32 [3072, 12, 64], P('data'), parts along dimension 0
- output 5: float32 [3072, 12, 64], P('data'), parts along dimension 0
- output 6: float32 [3072, 12, 64], P('data'), parts along dimension 0
- output 7: float32 [48, 64, 768], P('data'), parts along dimension 0
- output 8: float32 [3072], P('data'), parts along dimension 0
- output 9: float32 [3072, 2048], P('data'), parts along dimension 0
- output 10: float32 [3072, 2048], P('data'), parts along dimension 0
- output 11: float32 [8192, 768], P('data'), parts along dimension 0
There are 4 independent parts. A program takes and returns all parts, laid end to end along the dimension named above; an argument that names none is the same for every part.
All inputs are finite; a program needn't handle non-finite values.
Results may differ from a plain program's by a relative error of at most 0.0157877.
Values are sent between devices in bfloat16 or wider.
A program may use at most 768 MiB of HBM per device.

v0:
```python
import functools
import math

import jax
import jax.numpy as jnp
from jax import lax
from jax.experimental import pallas as pl
from jax.experimental.pallas import tpu as pltpu
from jax.sharding import PartitionSpec as P

F32 = jnp.float32
BF16 = jnp.bfloat16
LOG2E = math.log2(math.e)
VMEM = pltpu.VMEM
MESH = pl.DeviceIdType.MESH


def mm(a, b):
    return jnp.dot(a, b, preferred_element_type=F32)


def mm_bt(a, b):
    return lax.dot_general(a, b, (((1,), (1,)), ((), ())), preferred_element_type=F32)


def mm_at(a, b):
    return lax.dot_general(a, b, (((0,), (0,)), ((), ())), preferred_element_type=F32)


def rms_norm(tensor, gain):
    mean_sq = jnp.mean(tensor * tensor, axis=-1, keepdims=True)
    return tensor * lax.rsqrt(mean_sq + 1e-6) * gain


RIGHT, LEFT = 0, 1
DMA = pltpu.SemaphoreType.DMA

FWD_ORDER = [(0, 0), (0, 1), (1, 0), (1, 1), (-3, 0), (3, 1), (4, 0), (4, 1), (3, 0), (-3, 1), (2, 0), (-2, 1), (2, 1), (-2, 0), (-1, 1), (-1, 0)]
BWD_ORDER = [0, 1, 4, 3, -3, 2, -2, -1]
BWD_FIRST = 2
FWD_PLAN = {
    ("b", 0): [("y", 0, 1, 1), ("y", 1, 0, 1)],
    ("b", 11): [("y", 1, 1, 3), ("y", 1, 0, 3)],
    ("b", 12): [("go", 0, 0, 1)],
    ("b", 13): [("go", 1, 1, 1)],
    ("b", 14): [("o", 1, 0, 3)],
    ("b", 15): [("go", 0, 1, 1)],
    ("b", 17): [("o", 0, 1, 3)],
    ("b", 18): [("go", 1, 0, 1)],
    ("b", 20): [("o", 0, 0, 4)],
    ("b", 21): [("go", 1, 1, 2)],
    ("b", 23): [("o", 1, 1, 4)],
    ("b", 31): [("go", 0, 0, 2)],
    ("b", 32): [("go", 1, 0, 2)],
    ("b", 34): [("go", 0, 1, 2)],
    ("b", 35): [("go", 1, 1, 3)],
    ("b", 36): [("o", 0, 0, 3)],
    ("b", 37): [("o", 1, 1, 3)],
    ("b", 38): [("o", 0, 1, 2)],
    ("b", 4): [("y", 0, 0, 2), ("y", 1, 1, 2)],
    ("b", 40): [("go", 1, 0, 3)],
    ("b", 41): [("o", 1, 0, 2)],
    ("b", 42): [("go", 0, 1, 3)],
    ("b", 43): [("go", 1, 1, 4)],
    ("b", 8): [("y", 0, 1, 2), ("y", 1, 0, 2)],
    ("b", 9): [("go", "start")],
    ("r", 3): [("y", 0, 0, 3), ("y", 0, 1, 3)],
    ("r", 5): [("y", 0, 0, 4), ("y", 1, 1, 4)],
    ("s", 1): [("y", 0, 0, 1), ("y", 1, 1, 1)],
    ("t", 1): [("o", 0, 0, 2), ("o", 1, 1, 2), ("o", 0, 1, 1), ("o", 1, 0, 1), ("o", 0, 0, 1), ("o", 1, 1, 1), ("o", 0, 1, 0), ("o", 1, 0, 0), ("o", 0, 0, 0), ("o", 1, 1, 0)],
    ("t", 2): [("go", 0, 0, 3)],
    ("t", 6): [("go", 0, 0, 4)],
}
BWD_PLAN = {
    ("b", 1): [("dh", 0, 0, 1), ("dh", 1, 1, 1)],
    ("b", 11): [("dh", 0, 1, 3), ("dh", 1, 0, 3), ("st", 0, 0, 3), ("st", 1, 1, 3), ("st", 0, 1, 3), ("st", 1, 0, 3)],
    ("b", 12): [("dq0", 0, 0, 4)],
    ("b", 13): [("dq0", 1, 1, 4)],
    ("b", 14): [("att", 0, 0, 1), ("att", 1, 1, 1)],
    ("b", 15): [("dq0", 0, 1, 3), ("att", 0, 1, 1), ("att", 1, 0, 1)],
    ("b", 16): [("dq0", 0, 0, 3), ("dq0", 1, 0, 3)],
    ("b", 17): [("dq0", 1, 1, 3)],
    ("b", 18): [("att", 0, 0, 2), ("att", 1, 1, 2)],
    ("b", 19): [("dq0", 0, 1, 2), ("att", 1, 0, 2)],
    ("b", 2): [("dh", 0, 1, 1), ("dh", 1, 0, 1), ("st", 0, 0, 1), ("st", 1, 1, 1)],
    ("b", 20): [("dq0", 1, 0, 2), ("att", 0, 1, 2)],
    ("b", 21): [("dq0", 0, 0, 2), ("dq0", 1, 1, 2)],
    ("b", 22): [("att", 0, 0, 3), ("att", 1, 1, 3)],
    ("b", 23): [("dq0", 0, 1, 1), ("ar0", 0, 1, 3), ("ar0", 1, 0, 3), ("ar0", 0, 0, 4), ("ar0", 1, 1, 4), ("att", 1, 0, 3)],
    ("b", 24): [("dq0", 1, 0, 1), ("dq1", 0, 0, 4), ("att", 0, 1, 3)],
    ("b", 25): [("dq0", 0, 0, 1), ("dq0", 1, 1, 1), ("dq1", 1, 1, 4)],
    ("b", 27): [("dq1", 0, 1, 3), ("att", 0, 0, 4), ("att", 1, 1, 4)],
    ("b", 28): [("dq0", 0, 1, 0), ("dq1", 1, 0, 3), ("ar0", 1, 0, 2), ("ar0", 1, 1, 3), ("ar0", 0, 1, 2)],
    ("b", 29): [("dq0", 1, 0, 0), ("ar0", 0, 0, 3)],
    ("b", 3): [("st", 0, 1, 1), ("st", 1, 0, 1)],
    ("b", 30): [("dq0", 1, 1, 0), ("dq1", 0, 0, 3)],
    ("b", 31): [("dq0", 0, 0, 0), ("ds0", "start"), ("dq1", 1, 1, 3)],
    ("b", 32): [("dq1", 0, 1, 2), ("dq1", 1, 0, 2)],
    ("b", 33): [("ar0", 0, 1, 1), ("ar0", 1, 0, 1)],
    ("b", 34): [("ar0", 0, 0, 2), ("ar0", 1, 1, 2), ("ds0", 1, 1, 1)],
    ("b", 35): [("dq1", 0, 0, 2), ("dq1", 1, 1, 2), ("ar1", 0, 1, 3), ("ar1", 1, 0, 3), ("ar1", 0, 0, 4), ("ar1", 1, 1, 4), ("ds0", 1, 0, 1), ("ds0", 0, 0, 1), ("ds0", 0, 1, 1)],
    ("b", 36): [("dq1", 0, 1, 1), ("dq1", 1, 0, 1), ("dq2", 0, 0, 4), ("ar0", 0, 1, 0), ("ar0", 1, 0, 0)],
    ("b", 37): [("dq2", 1, 1, 4), ("ar0", 0, 0, 1), ("ar0", 1, 1, 1)],
    ("b", 38): [("dq1", 0, 0, 1), ("ds0", 1, 1, 2)],
    ("b", 39): [("dq1", 1, 1, 1), ("dq2", 0, 1, 3), ("ar1", 0, 1, 2)],
    ("b", 40): [("dq2", 1, 0, 3), ("ar1", 1, 0, 2), ("ar1", 0, 0, 3), ("ar1", 1, 1, 3), ("ds0", 0, 0, 2)],
    ("b", 41): [("ds0", 0, 1, 2), ("ds0", 1, 0, 2)],
    ("b", 42): [("dq1", 0, 1, 0), ("dq1", 1, 0, 0)],
    ("b", 43): [("dq2", 0, 0, 3), ("dq2", 1, 1, 3)],
    ("b", 44): [("ar0", 0, 0, 0), ("ar0", 1, 1, 0), ("as0", "start"), ("ds0", 1, 1, 3)],
    ("b", 45): [("dq1", 0, 0, 0), ("dq1", 1, 1, 0), ("ds1", "start")],
    ("b", 46): [("dq2", 0, 1, 2), ("dq2", 1, 0, 2), ("ar1", 0, 1, 1)],
    ("b", 47): [("ar1", 1, 0, 1), ("ar1", 0, 0, 2), ("ar1", 1, 1, 2), ("ar2", 0, 1, 3), ("ar2", 1, 0, 3), ("ar2", 0, 0, 4), ("ar2", 1, 1, 4), ("ds0", 0, 0, 3), ("ds0", 0, 1, 3), ("ds0", 1, 0, 3)],
    ("b", 5): [("dh", 0, 0, 2), ("dh", 1, 1, 2)],
    ("b", 7): [("dh", 0, 1, 2), ("dh", 1, 0, 2), ("st", 0, 0, 2), ("st", 1, 1, 2), ("st", 0, 1, 2), ("st", 1, 0, 2)],
    ("b", 9): [("dh", 0, 0, 3), ("dh", 1, 1, 3)],
    ("f", 0): [("ar1", 1, 0, 0), ("ar1", 0, 0, 1), ("ar1", 1, 1, 1), ("ar2", 0, 1, 2)],
    ("f", 11): [("dq2", 0, 1, 0), ("dq2", 1, 0, 0)],
    ("f", 13): [("ar1", 0, 0, 0), ("ar1", 1, 1, 0), ("as1", "start")],
    ("f", 14): [("ar2", 0, 1, 1), ("ar2", 1, 0, 1)],
    ("f", 16): [("ar2", 0, 0, 2), ("ar2", 1, 1, 2)],
    ("f", 17): [("dq2", 0, 0, 0), ("dq2", 1, 1, 0), ("ds2", "start"), ("as0", 0, 0, 3), ("as0", 1, 1, 3)],
    ("f", 18): [("as0", 0, 1, 3), ("as0", 1, 0, 3)],
    ("f", 19): [("ds1", 0, 0, 3), ("ds1", 1, 1, 3)],
    ("f", 2): [("ar2", 1, 0, 2), ("ar2", 0, 0, 3)],
    ("f", 21): [("ds1", 0, 1, 3), ("ds1", 1, 0, 3)],
    ("f", 23): [("as1", 0, 0, 1), ("as1", 1, 1, 1)],
    ("f", 25): [("as1", 0, 1, 1), ("as1", 1, 0, 1)],
    ("f", 26): [("ar2", 0, 1, 0), ("ar2", 1, 0, 0), ("ar2", 0, 0, 1), ("ar2", 1, 1, 1), ("ds2", 0, 0, 1), ("ds2", 1, 1, 1), ("ds2", 0, 1, 1), ("ds2", 1, 0, 1)],
    ("f", 28): [("as0", 0, 0, 4), ("as0", 1, 1, 4)],
    ("f", 3): [("ar2", 1, 1, 3), ("ds0", 0, 0, 4)],
    ("f", 30): [("ds1", 0, 0, 4), ("ds1", 1, 1, 4)],
    ("f", 32): [("as1", 0, 0, 2), ("as1", 1, 1, 2)],
    ("f", 34): [("as1", 0, 1, 2), ("as1", 1, 0, 2)],
    ("f", 35): [("ar2", 0, 0, 0), ("ar2", 1, 1, 0), ("as2", "start"), ("ds2", 0, 0, 2), ("ds2", 1, 1, 2), ("ds2", 0, 1, 2), ("ds2", 1, 0, 2)],
    ("f", 6): [("dq2", 0, 0, 1), ("dq2", 1, 1, 1)],
    ("f", 8): [("as0", 0, 0, 2), ("as0", 1, 1, 2), ("as0", 0, 1, 2), ("as0", 1, 0, 2), ("ds1", 0, 0, 2), ("ds1", 1, 1, 2), ("ds1", 0, 1, 2), ("ds1", 1, 0, 2)],
    ("h", 0): [("dq2", 0, 0, 2), ("dq2", 1, 1, 2)],
    ("h", 1): [("as0", 0, 0, 1), ("as0", 1, 1, 1)],
    ("h", 3): [("as0", 0, 1, 1), ("as0", 1, 0, 1), ("ds0", 1, 1, 4), ("ds1", 0, 0, 1)],
    ("h", 4): [("ds1", 0, 1, 1), ("ds1", 1, 1, 1)],
    ("h", 5): [("ds1", 1, 0, 1)],
    ("h", 6): [("dq2", 0, 1, 1)],
    ("h", 7): [("dq2", 1, 0, 1), ("ar1", 0, 1, 0)],
    ("m", 0): [("as1", 0, 0, 3), ("as1", 1, 1, 3), ("as1", 0, 1, 3), ("as1", 1, 0, 3)],
    ("m", 2): [("as2", 0, 0, 1), ("as2", 1, 1, 1)],
    ("m", 3): [("as2", 0, 1, 1), ("as2", 1, 0, 1)],
    ("m", 4): [("ds2", 0, 0, 3), ("ds2", 1, 1, 3), ("ds2", 0, 1, 3), ("ds2", 1, 0, 3), ("ds2", 0, 0, 4), ("ds2", 1, 1, 4)],
    ("q", 0): [("as1", 0, 0, 4), ("as1", 1, 1, 4), ("as2", 0, 0, 2), ("as2", 1, 1, 2), ("as2", 0, 1, 2), ("as2", 1, 0, 2)],
    ("q", 6): [("as2", 0, 0, 3), ("as2", 1, 1, 3)],
    ("q", 8): [("as2", 0, 1, 3), ("as2", 1, 0, 3), ("as2", 0, 0, 4), ("as2", 1, 1, 4)],
    ("r", 12): [("dh", 0, 0, 4), ("dh", 1, 1, 4), ("att", "start"), ("st", 0, 0, 4), ("st", 1, 1, 4)],
}


class Ring:
    def __init__(self, chips):
        me = lax.axis_index('seq')
        self.chips = chips
        self.far = chips // 2
        self.z = me // 2
        self.core = me - 2 * self.z
        self.partner = 2 * self.z + 1 - self.core
        self.next = (2 * self.chip(1) + self.core, 2 * self.chip(-1) + self.core)
        self.hops = {(RIGHT, 0): self.far, (LEFT, 1): self.far, (RIGHT, 1): self.far - 1, (LEFT, 0): self.far - 1}

    def chip(self, off):
        return lax.rem(self.z + off + self.chips, self.chips)

    def ahead(self, d, k):
        return self.chip(k if d == RIGHT else -k)

    def enter(self):
        barrier = pltpu.get_barrier_semaphore()
        for dev in (self.partner,) + self.next:
            pl.semaphore_signal(barrier, inc=1, device_id={'seq': dev}, device_id_type=MESH)
        pl.semaphore_wait(barrier, 3)


def remote(src, dst, ssem, rsem, dev):
    return pltpu.make_async_remote_copy(src_ref=src, dst_ref=dst, send_sem=ssem, recv_sem=rsem, device_id={'seq': dev}, device_id_type=MESH)


def sent(every, ssem, rsem, dev):
    remote(every, every, ssem, rsem, dev).wait_send()


class Share:
    def __init__(self, ring, buf, src, sems):
        self.ring, self.buf, self.src = ring, buf, src
        self.ss, self.rs = sems

    def slot(self, chip, half):
        return self.buf.at[chip, half]

    def send(self, d, half, t):
        slot = self.slot(self.ring.ahead(d, 1 - t), half)
        src = self.src(half) if t == 1 else slot
        return remote(src, slot, self.ss.at[0], self.rs.at[d, half, t - 1], self.ring.next[d])

    def recv(self, d, half, t):
        slot = self.slot(self.ring.ahead(d, -t), half)
        return remote(slot, slot, self.ss.at[0], self.rs.at[d, half, t - 1], self.ring.next[d])

    def start(self):
        for d, half in self.ring.hops:
            self.send(d, half, 1).start()

    def came(self, d, half, t):
        pass

    def move(self, d, half, t):
        self.recv(d, half, t).wait_recv()
        if t < self.ring.hops[d, half]:
            self.send(d, half, t + 1).start()
        self.came(d, half, t)

    def drain(self):
        sent(self.buf.at[pl.ds(0, self.ring.chips - 1)], self.ss.at[0], self.rs.at[0, 0, 0], self.ring.next[0])


class Rows(Share):
    def __init__(self, ring, buf, src, sems):
        super().__init__(ring, buf, src, sems[:2])
        self.fs, self.fr, self.os, self.orr = sems[2:]

    def slot(self, chip, half):
        return self.buf.at[chip, self.ring.core, half]

    def pslot(self, chip, half):
        return self.buf.at[chip, 1 - self.ring.core, half]

    def start(self):
        super().start()
        for half in range(2):
            self.own(half).start()

    def own(self, half):
        return remote(self.src(half), self.slot(self.ring.z, half), self.os.at[0], self.orr.at[half], self.ring.partner)

    def forward(self, d, half, t):
        slot = self.slot(self.ring.ahead(d, -t), half)
        return remote(slot, slot, self.fs.at[0], self.fr.at[d, half, t - 1], self.ring.partner)

    def came(self, d, half, t):
        self.forward(d, half, t).start()

    def ready(self, off):
        ring = self.ring
        if off == 0:
            for half in range(2):
                slot = self.pslot(ring.z, half)
                remote(slot, slot, self.os.at[0], self.orr.at[half], ring.partner).wait_recv()
            return
        for (d, half), n in ring.hops.items():
            t = ring.far if abs(off) == ring.far else (-off if d == RIGHT else off)
            if 1 <= t <= n:
                slot = self.pslot(ring.ahead(d, -t), half)
                remote(slot, slot, self.fs.at[0], self.fr.at[d, half, t - 1], ring.partner).wait_recv()

    def drain(self):
        every = self.buf.at[pl.ds(0, self.ring.chips - 1), 0]
        sent(every, self.ss.at[0], self.rs.at[0, 0, 0], self.ring.next[0])
        sent(every, self.fs.at[0], self.fr.at[0, 0, 0], self.ring.partner)
        sent(self.buf.at[0, 0], self.os.at[0], self.orr.at[0], self.ring.partner)


class Reduce:
    def __init__(self, ring, part, rbuf, merge, sems):
        self.ring, self.part, self.rbuf, self.merge = ring, part, rbuf, merge
        self.ss, self.rs = sems

    def send(self, d, half, o):
        return remote(self.part.at[self.ring.ahead(d, o), half], self.rbuf.at[d, half, o - 1], self.ss.at[0], self.rs.at[d, half, o - 1], self.ring.next[d])

    def recv(self, d, half, o):
        slot = self.rbuf.at[d, half, o]
        return remote(slot, slot, self.ss.at[0], self.rs.at[d, half, o], self.ring.next[d])

    def move(self, d, half, o):
        if o < self.ring.hops[d, half]:
            self.recv(d, half, o).wait_recv()
            self.merge(self.part.at[self.ring.ahead(d, o), half], self.rbuf.at[d, half, o])
        if o > 0:
            self.send(d, half, o).start()

    def drain(self):
        sent(self.part.at[pl.ds(0, self.ring.chips - 1)], self.ss.at[0], self.rs.at[0, 0, 0], self.ring.next[0])


def pick(i, values):
    out = jnp.int32(values[-1])
    for k, v in enumerate(values[:-1]):
        out = jnp.where(i == k, jnp.int32(v), out)
    return out


def mask_lanes(ref, len_ref, start):
    row = lax.broadcasted_iota(jnp.int32, ref.shape, 0) + start
    lane = lax.broadcasted_iota(jnp.int32, ref.shape, 1)
    bias = jnp.where(row < len_ref[0], 0.0, -1e30)
    ref[...] = jnp.where(lane == 0, bias, jnp.where(lane < 4, 1.0, 0.0)).astype(BF16)


def dispatch(index, table):
    def branch(keys):
        if len(keys) == 1:
            def run():
                for fn in table[keys[0]]:
                    fn()
            pl.when(index == keys[0])(run)
            return
        low, high = keys[:len(keys) // 2], keys[len(keys) // 2:]
        pl.when(index < high[0])(functools.partial(branch, low))
        pl.when(index >= high[0])(functools.partial(branch, high))
    if table:
        branch(sorted(table))


def add_into(dst, src):
    dst[...] = dst[...] + src[...]


def parts3(x):
    hi = x.astype(BF16)
    rest = x - hi.astype(F32)
    mid = rest.astype(BF16)
    lo = (rest - mid.astype(F32)).astype(BF16)
    return hi, mid, lo


def bwd_kernel(dims, len_ref, dh_ref, own_ref, gn_ref, att_ref, g_ref,
               k_hbm, v_hbm, kt_hbm, qz_hbm, wo_hbm, wq_hbm, wk_hbm, wv_hbm, ma_hbm, mb_hbm, y_hbm, gog, wg_hbm, wu_hbm, wd_hbm,
               gvec_ref, dqo_ref, gmem, gwk, gwv, gwq, gwo, gdown, ggate, gup, attg,
               k_ref, v_ref, kt_ref, qz_ref, wo_ref, wq_ref, wk_ref, wv_ref, ak_ref,
               dhg, doz, aqs, ads, stb, dk, dv, dkv, dkvp, dqp, dqr, dqa, arp, arr, ara, pvec, pdq, spb,
               msc, ybuf, abuf, wbuf, dbuf, wt, gst, gsw, gwo_s, gwq_s,
               *sems):
    chips, rows, mem, dim, hc, c, ff = dims
    QT = 2 * rows
    T = 2 * mem
    MC = min(256, mem)
    nm = T // MC
    inner = hc * 64
    np_ = hc // 2
    seg = 256 // chips // 2
    fh = ff // 2
    FT = wt.shape[1]
    nf = fh // FT
    ring = Ring(chips)
    z, core, far = ring.z, ring.core, ring.far
    sems = list(sems)

    def take(n):
        out = sems[:n]
        del sems[:n]
        return out

    half_rows = rows // 2
    part_ = functools.partial
    rsrc = lambda ref: (lambda half: ref.at[pl.ds(half * half_rows, half_rows)])
    dh_g = Rows(ring, dhg, rsrc(dh_ref), take(6))
    att_g = Rows(ring, attg, rsrc(att_ref), take(6))
    st_g = Share(ring, stb, lambda half: stb.at[z, half], take(2))
    dq_r = [Reduce(ring, dqp.at[p], dqr.at[p], add_into, take(2)) for p in range(np_)]
    dq_s = [Share(ring, dqa.at[p], lambda half, p=p: dqa.at[p, z, half], take(2)) for p in range(np_)]
    ar_r = [Reduce(ring, arp.at[p], arr.at[p], add_into, take(2)) for p in range(np_)]
    ar_s = [Share(ring, ara.at[p], lambda half, p=p: ara.at[p, z, half], take(2)) for p in range(np_)]
    xs, xr, ls, gs, gr, gl, wsem, ysem, lsem = take(9)
    loads = [pltpu.make_async_copy(src, dst, lsem.at[n]) for n, (src, dst) in enumerate((
        (wo_hbm, wo_ref), (k_hbm, k_ref), (v_hbm, v_ref), (kt_hbm, kt_ref), (qz_hbm, qz_ref),
        (ma_hbm, msc.at[0, pl.ds(0, mem)]), (mb_hbm, msc.at[1, pl.ds(0, mem)]), (wq_hbm, wq_ref), (wk_hbm, wk_ref), (wv_hbm, wv_ref)))]
    for cp in loads:
        cp.start()
    ring.enter()
    dh_g.start()
    locals_ = [pltpu.make_async_copy(att_ref.at[pl.ds(half * half_rows, half_rows)], attg.at[z, core, half], ls.at[half]) for half in range(2)]
    for cp in locals_:
        cp.start()
    for half in range(2):
        dhg[z, core, half] = dh_ref[half * half_rows:(half + 1) * half_rows, :]
    doz[...] = jnp.zeros_like(doz)
    mask_lanes(ak_ref, len_ref, z * T)
    hrow = pl.ds(pl.multiple_of(core * inner, inner), inner)
    hcol = pl.ds(pl.multiple_of(core * inner, 128), inner)
    other_cols = pl.ds(pl.multiple_of((1 - core) * mem, mem), mem)
    my_cols = pl.ds(pl.multiple_of(core * mem, mem), mem)
    qmine = pl.ds(pl.multiple_of(core * rows, rows), rows)
    qother = pl.ds(pl.multiple_of((1 - core) * rows, rows), rows)

    def lanes(chip):
        return pl.ds(pl.multiple_of(chip * QT, QT), QT)

    def d_out(chip):
        return mm_bt(wo_ref[hrow, :], dhg[chip].reshape(QT, dim))

    def prepare(chip, dot=None):
        dot = d_out(chip) if dot is None else dot
        dob = dot.astype(BF16)
        q = lanes(chip)
        row = lax.broadcasted_iota(jnp.int32, (16, QT), 0)
        for h in range(hc):
            lo = h * 128 + (h % 2) * 64
            doz[lo:lo + 64, q] = dob[h * 64:(h + 1) * 64]
            for ref, half, first in ((aqs, 0, 1.0), (ads, 1, 0.0)):
                a, b, e = (x.astype(F32) for x in parts3(stb[chip, half, h:h + 1, :]))
                ref[h * 16:(h + 1) * 16, q] = jnp.where(row == 0, first, jnp.where(row == 1, a, jnp.where(row == 2, b, jnp.where(row == 3, e, 0.0)))).astype(BF16)

    dh_g.ready(0)
    loads[0].wait()
    dot0 = d_out(z)
    prod = dot0 * own_ref[:inner, :]
    for h in range(hc):
        stb[z, 0, h:h + 1, :] = -own_ref[inner + h:inner + h + 1, :]
        stb[z, 1, h:h + 1, :] = -jnp.sum(prod[h * 64:(h + 1) * 64], axis=0, keepdims=True)
    stb[z, 0, hc:8, :] = gn_ref[0:8 - hc, :]
    stb[z, 1, hc:8, :] = gn_ref[8 - hc:16 - 2 * hc, :]
    st_g.start()
    prepare(z, dot0)
    dk[...] = jnp.zeros_like(dk)
    dv[...] = jnp.zeros_like(dv)
    for cp in loads[1:]:
        cp.wait()

    def tile(h, chip):
        pair = h // 2
        q = lanes(chip)
        hz = pl.ds(pl.multiple_of(h * 128, 128), 128)
        h16 = pl.ds(pl.multiple_of(h * 16, 16), 16)
        ps = pl.ds(pl.multiple_of(pair * 128, 128), 128)
        hz64 = pl.ds(pl.multiple_of(h * 128 + (h - 2 * pair) * 64, 64), 64)
        h64 = pl.ds(pl.multiple_of(h * 64, 64), 64)
        hr = h64
        q_t = qz_ref[hz64, q]
        do_t = doz[hz64, q]
        r1 = jnp.concatenate([qz_ref[hz, q], aqs[h16, q]], axis=0)
        r2 = jnp.concatenate([doz[hz, q], ads[h16, q]], axis=0)
        stage = {}
        dq = None
        for j in range(nm + 2):
            if j < nm:
                r = slice(j * MC, (j + 1) * MC)
                ak = ak_ref[r, 0:16]
                stage["a", j] = (mm(jnp.concatenate([k_ref[r, ps], ak], axis=1), r1), mm(jnp.concatenate([v_ref[r, ps], ak], axis=1), r2))
            if 1 <= j <= nm:
                s, dp = stage.pop(("a", j - 1))
                a = jnp.exp2(s * c)
                stage["b", j - 1] = (a.astype(BF16), (a * dp).astype(BF16))
            if j >= 2:
                r = slice((j - 2) * MC, (j - 1) * MC)
                pb, ds = stage.pop(("b", j - 2))
                dv[hr, r] += mm_bt(do_t, pb)
                dk[hr, r] += mm_bt(q_t, ds)
                d = mm(kt_ref[h64, r], ds)
                dq = d if dq is None else dq + d
        dqp[pair, chip, h - 2 * pair] = dq

    scale = 0.125

    def xp(p):
        return remote(dkv.at[p, :, other_cols], dkvp.at[p], xs.at[p], xr.at[p], ring.partner)

    def xq(p):
        return remote(dqa.at[p, z, :, :, qother], pdq.at[p], xs.at[np_ + p], xr.at[np_ + p], ring.partner)

    def share_dq(p):
        for half in range(2):
            dqa[p, z, half] = (dqp[p, z, half] * scale).astype(BF16)
        dq_s[p].start()
        xq(p).start()

    def share_ar(p):
        for half in range(2):
            ara[p, z, half] = arp[p, z, half]
        ar_s[p].start()

    moves = {"dh": dh_g, "st": st_g, "att": att_g}
    begins = {"att": att_g.start}
    for p in range(np_):
        moves.update({f"dq{p}": dq_r[p], f"ds{p}": dq_s[p], f"ar{p}": ar_r[p], f"as{p}": ar_s[p]})
        begins.update({f"ds{p}": part_(share_dq, p), f"as{p}": part_(share_ar, p)})

    def acts(*point):
        return [begins[e[0]] if e[1] == "start" else part_(moves[e[0]].move, *e[1:]) for e in BWD_PLAN.get(point, [])]

    def run(*point):
        for fn in acts(*point):
            fn()

    def table(kind, n):
        return {k: acts(kind, k) for k in range(n) if acts(kind, k)}

    offs = BWD_ORDER
    first = BWD_FIRST * hc
    per = 2 * (chips - BWD_FIRST)
    needs = {k * hc: offs[k] for k in range(1, BWD_FIRST)}
    needs.update({first + 2 * (k - BWD_FIRST): offs[k] for k in range(BWD_FIRST, chips)})

    def project(p):
        r = pl.ds(pl.multiple_of(p * 128, 128), 128)
        dkv[p, 0:128, :] = (dk[r, :] * scale).astype(BF16)
        dkv[p, 128:256, :] = dv[r, :].astype(BF16)
        xp(p).start()
        g = mm(dkv[p, :, my_cols], msc[0, 0:mem]) + mm(dkv[p, :, other_cols], msc[1, 0:mem])
        for n in range(2 * chips):
            arp[p, n // 2, n % 2] = g[n * seg:(n + 1) * seg]

    def body(it, carry):
        early = it < first
        b = it - first
        p = b // per
        r = b - p * per
        h = jnp.where(early, it % hc, 2 * p + r % 2)
        chip = ring.chip(pick(jnp.where(early, it // hc, BWD_FIRST + r // 2), offs))
        dispatch(it, {k: acts("r", k) + [part_(dh_g.ready, off)] for k, off in needs.items()})
        fresh = (early & (it > 0) & (it % hc == 0)) | ((b >= 0) & (b < per) & (r % 2 == 0))
        pl.when(fresh)(part_(prepare, chip))
        tile(h, chip)
        pl.when((b >= 0) & (r == per - 1))(part_(project, p))
        dispatch(it, table("b", chips * hc))
        return carry

    lax.fori_loop(0, chips * hc, body, 0)
    run("p", np_)
    near = range(1 - far, far + 1)

    for cp in locals_:
        cp.wait()
    for off in near:
        att_g.ready(off)
    gain2 = g_ref[1:2, :].astype(F32)
    gwo_s[...] = jnp.zeros_like(gwo_s)

    def y_fetch(ch, slot):
        return pltpu.make_async_copy(y_hbm.at[ch], ybuf.at[slot], ysem.at[slot, 0])

    def fetch(ch, slot):
        return (y_fetch(ch, slot), pltpu.make_async_copy(attg.at[ch], abuf.at[slot], ysem.at[slot, 1]))

    for cp in fetch(0, 0):
        cp.start()

    def hidden(ch, carry):
        slot = ch % 2
        for cp in fetch(ch, slot):
            cp.wait()

        @pl.when(ch + 1 < chips)
        def _():
            for cp in fetch(ch + 1, 1 - slot):
                cp.start()
        att = abuf[slot].reshape(QT, dim)
        h = (ybuf[slot].reshape(QT, dim).astype(F32) + mm(att, wo_ref[...])).astype(BF16)
        qz_ref[0:dim, lanes(ch)] = rms_norm(h.astype(F32), gain2).astype(BF16).T
        ah = jnp.where(core == 0, att[:, :inner], att[:, inner:])
        gwo_s[...] += mm_at(ah, dhg[ch].reshape(QT, dim))
        dispatch(ch, table("h", chips))
        return carry

    lax.fori_loop(0, chips, hidden, 0)
    dh_g.drain()
    go_load = pltpu.make_async_copy(gog, dhg, ls.at[0])
    go_load.start()

    def partner_block(buf, dst, k):
        return pltpu.make_async_copy(buf, dst, gl.at[k]), remote(buf, dst, gs.at[k], gr.at[k], ring.partner)

    def both_start(pair):
        pair[0].start()
        pair[1].start()

    def both_wait(pair):
        pair[0].wait()
        pair[1].wait()

    wo_out = partner_block(gwo_s, gwo.at[hrow], 3 * nf)
    both_start(wo_out)

    def w_fetch(f, slot):
        cols = pl.ds(pl.multiple_of(core * fh + f * FT, FT), FT)
        return (pltpu.make_async_copy(wg_hbm.at[:, cols], wbuf.at[slot, 0], wsem.at[slot, 0]),
                pltpu.make_async_copy(wu_hbm.at[:, cols], wbuf.at[slot, 1], wsem.at[slot, 1]),
                pltpu.make_async_copy(wd_hbm.at[cols], dbuf.at[slot], wsem.at[slot, 2]))

    for cp in w_fetch(0, 0):
        cp.start()
    go_load.wait()
    f_table = table("f", 9 * nf)

    def block(f, n):
        if n == 0:
            return partner_block(gst.at[0, pl.ds(0, FT)], gdown.at[pl.ds(pl.multiple_of(core * fh + f * FT, FT), FT)], f)
        return partner_block(gsw.at[n - 1], (ggate, gup)[n - 1].at[:, pl.ds(pl.multiple_of(core * fh + f * FT, FT), FT)], n * nf + f)

    def mlp(f, carry):
        slot = f % 2
        for cp in w_fetch(f, slot):
            cp.wait()

        @pl.when(f + 1 < nf)
        def _():
            for cp in w_fetch(f + 1, 1 - slot):
                cp.start()
        for n in range(2):
            wt[n] = wbuf[slot, n].T

        def act_chunk(ch, cc):
            q = lanes(ch)
            n2t = qz_ref[0:dim, q]
            g = mm(wt[0], n2t)
            u = mm(wt[1], n2t)
            ga = mm_bt(dbuf[slot], dhg[ch].reshape(QT, dim))
            sig = jax.nn.sigmoid(g)
            si = g * sig
            doz[0:FT, q] = (si * u).astype(BF16)
            doz[FT:2 * FT, q] = (ga * u * (sig + si * (1.0 - sig))).astype(BF16)
            doz[2 * FT:3 * FT, q] = (ga * si).astype(BF16)
            dispatch(f * 9 + ch, f_table)
            return cc

        lax.fori_loop(0, chips, act_chunk, 0)

        @pl.when(f > 0)
        def _():
            for n in range(3):
                both_wait(block(f - 1, n))
        acc = [None] * 3
        for ch in range(chips):
            q = slice(ch * QT, (ch + 1) * QT)
            n2t = qz_ref[0:dim, q]
            for n, d in enumerate((mm(doz[0:FT, q], dhg[ch].reshape(QT, dim)), mm_bt(n2t, doz[FT:2 * FT, q]), mm_bt(n2t, doz[2 * FT:3 * FT, q]))):
                acc[n] = d if acc[n] is None else acc[n] + d
        gst[0, 0:FT] = acc[0]
        gsw[0] = acc[1]
        gsw[1] = acc[2]
        for n in range(3):
            both_start(block(f, n))
        dispatch(f * 9 + 8, f_table)
        return carry

    lax.fori_loop(0, nf, mlp, 0)
    for p in range(np_):
        remote(dkvp.at[p], dkvp.at[p], xs.at[p], xr.at[p], ring.partner).wait_recv()
    nb = 4
    w = mem // nb
    for n in range(3):
        both_wait(block(nf - 1, n))

    def gm(b):
        return pltpu.make_async_copy(gst.at[b % 2, pl.ds(0, w)], gmem.at[pl.ds(pl.multiple_of(b * w, w), w)], gl.at[3 * nf + 2 + b % 2])

    def memory_rows(b, carry):
        @pl.when(b > 1)
        def _():
            gm(b - 2).wait()
        cb = pl.ds(pl.multiple_of(core * mem + b * w, w), w)
        cp = pl.ds(pl.multiple_of(b * w, w), w)
        acc = None
        for p in range(np_):
            own_e = pl.ds(pl.multiple_of(core * inner + p * 128, 128), 128)
            oth_e = pl.ds(pl.multiple_of((1 - core) * inner + p * 128, 128), 128)
            for part, w_ref in ((0, wk_ref), (1, wv_ref)):
                e = slice(part * 128, (part + 1) * 128)
                lhs = jnp.concatenate([dkv[p, e, cb], dkvp[p, e, cp]], axis=0)
                rhs = jnp.concatenate([w_ref[:, own_e], w_ref[:, oth_e]], axis=1)
                d = mm_bt(lhs.T, rhs)
                acc = d if acc is None else acc + d
        gst[b % 2, 0:w] = acc
        gm(b).start()
        dispatch(b, table("m", nb))
        return carry

    lax.fori_loop(0, nb, memory_rows, 0)
    run("m", nb)

    gain = g_ref[0:1, :].astype(F32)
    y_fetch(0, 0).start()
    spb[...] = jnp.zeros_like(spb)
    gwq_s[...] = jnp.zeros_like(gwq_s)
    wq_h = wq_ref[:, hcol]

    def query(ch, carry):
        slot = ch % 2
        y_fetch(ch, slot).wait()

        @pl.when(ch + 1 < chips)
        def _():
            y_fetch(ch + 1, 1 - slot).start()
        x = ybuf[slot].reshape(QT, dim).astype(F32)
        xhat = x * lax.rsqrt(jnp.mean(x * x, axis=-1, keepdims=True) + 1e-6)
        n1 = (xhat * gain).astype(BF16)
        dqc = jnp.concatenate([dqa[p, ch].reshape(128, QT) for p in range(np_)], axis=0)
        dn = mm_bt(dqc.T, wq_h)
        gwq_s[...] += mm(dqc, n1)
        spb[0:1, :] += jnp.sum(dn * xhat, axis=0, keepdims=True)
        dispatch(ch, table("q", chips))
        return carry

    lax.fori_loop(0, chips, query, 0)
    gvec2 = jnp.zeros((16 - 2 * hc, QT), F32)
    for ch in range(chips):
        gvec2 = gvec2 + jnp.concatenate([stb[ch, 0, hc:8, :], stb[ch, 1, hc:8, :]], axis=0)
    for n in range(dim // QT):
        spb[1:2, n * QT:(n + 1) * QT] = gvec2[n:n + 1]
    cv = remote(spb, pvec, xs.at[2 * np_], xr.at[2 * np_], ring.partner)
    cv.start()
    wq_out = partner_block(gwq_s, gwq.at[hrow], 3 * nf + 1)
    both_start(wq_out)
    for p in range(np_):
        own_r = pl.ds(pl.multiple_of(core * inner + p * 128, 128), 128)
        oth_r = pl.ds(pl.multiple_of((1 - core) * inner + p * 128, 128), 128)
        dqo_ref[own_r, :] = dqa[p, z, :, :, qmine].reshape(128, rows)
        xq(p).wait()
        dqo_ref[oth_r, :] = pdq[p].reshape(128, rows)
    run("q", chips)
    wkv_out = []
    for p in range(np_):
        for k, out in enumerate((gwk, gwv)):
            n = 2 * p + k
            src = ara.at[p, pl.ds(k * (chips // 2), chips // 2)]
            wkv_out.append(pltpu.make_async_copy(src, out.at[core, p], ls.at[2 + n]))
            wkv_out.append(remote(src, out.at[core, p], xs.at[2 * np_ + 1 + n], xr.at[2 * np_ + 1 + n], ring.partner))
    for cp in wkv_out:
        cp.start()
    for p in range(np_):
        xp(p).wait_send()
    cv.wait()
    gvec_ref[...] = spb[0:2] + pvec[0:2]
    both_wait(wo_out)
    both_wait(wq_out)
    for cp in wkv_out:
        cp.wait()
    for b in range(nb - 2, nb):
        gm(b).wait()
    for obj in [att_g, st_g] + dq_r + dq_s + ar_r + ar_s:
        obj.drain()


def bwd_call(dims, *args):
    chips, rows, mem, dim, hc, c, ff = dims
    inner = hc * 64
    QT = 2 * rows
    T = 2 * mem
    np_ = hc // 2
    h2 = chips // 2
    seg = 256 // chips // 2
    FT = ff // 8
    v = pl.BlockSpec(memory_space=VMEM)
    hbm = pl.BlockSpec(memory_space=pl.ANY)
    s3 = (2, 2, h2)
    rows_sems = [DMA((1,)), DMA(s3)] * 2 + [DMA((1,)), DMA((2,))]
    two = [DMA((1,)), DMA(s3)]
    S = jax.ShapeDtypeStruct
    gshape = (chips, 2, 2, rows // 2, dim)
    cols = chips * QT
    wsq = VMEM((dim, 2 * inner), BF16)
    return pl.pallas_call(
        functools.partial(bwd_kernel, dims),
        out_shape=(S((2, dim), F32), S((2 * inner, rows), BF16), S((mem, dim), F32), S((2, np_, chips // 2, 2, seg, dim), F32), S((2, np_, chips // 2, 2, seg, dim), F32), S((2 * inner, dim), F32), S((2 * inner, dim), F32),
                   S((ff, dim), F32), S((dim, ff), F32), S((dim, ff), F32), S(gshape, BF16)),
        in_specs=[pl.BlockSpec(memory_space=pltpu.SMEM)] + [v] * 5 + [hbm] * 15, out_specs=(v,) * 2 + (hbm,) * 9,
        scratch_shapes=[
            VMEM((T, inner), BF16), VMEM((T, inner), BF16), VMEM((inner, T), BF16), VMEM((hc * 128, cols), BF16), VMEM((2 * inner, dim), BF16), wsq, wsq, wsq, VMEM((T, 128), BF16),
            VMEM(gshape, BF16), VMEM((max(hc * 128, 3 * FT), cols), BF16), VMEM((hc * 16, cols), BF16), VMEM((hc * 16, cols), BF16),
            VMEM((chips, 2, 8, QT), F32), VMEM((inner, T), F32), VMEM((inner, T), F32), VMEM((np_, 256, T), BF16), VMEM((np_, 256, mem), BF16),
            VMEM((np_, chips, 2, 64, QT), F32), VMEM((np_, 2, 2, h2, 64, QT), F32), VMEM((np_, chips, 2, 64, QT), BF16),
            VMEM((np_, chips, 2, seg, dim), F32), VMEM((np_, 2, 2, h2, seg, dim), F32), VMEM((np_, chips, 2, seg, dim), F32),
            VMEM((8, dim), F32), VMEM((np_, 2, 64, rows), BF16), VMEM((8, dim), F32),
            VMEM((2, mem, dim), BF16), VMEM((2, 2, 2, rows // 2, dim), BF16), VMEM((2, 2, 2, rows // 2, dim), BF16),
            VMEM((2, 2, dim, FT), BF16), VMEM((2, FT, dim), BF16), VMEM((2, FT, dim), BF16), VMEM((2, max(FT, mem // 4), dim), F32), VMEM((2, dim, FT), F32),
            VMEM((inner, dim), F32), VMEM((inner, dim), F32)]
        + rows_sems * 2 + two * (1 + 4 * np_) + [DMA((4 * np_ + 1,))] * 2 + [DMA((2 + 2 * np_,)), DMA((14,)), DMA((14,)), DMA((16,)), DMA((2, 3)), DMA((2, 2)), DMA((10,))],
        compiler_params=pltpu.CompilerParams(vmem_limit_bytes=66_900_000, collective_id=1, has_side_effects=True),
        cost_estimate=pl.CostEstimate(flops=10**10, bytes_accessed=30 << 20, transcendentals=0),
        name="attn_bwd")(*args)


def fwd_kernel(dims, len_ref, y_ref, go_ref, m_ref, g_ref, wq_hbm, wk_hbm, wv_hbm, wo_hbm, wg_hbm, wu_hbm, wd_hbm,
               own, att_ref, dh_ref, gh_ref, gn_ref, k_out, v_out, kt_out, qz_out, mg_out, yall, gog,
               k_s, v_s, kt_s, qz, mg, wq_ref, wk_ref, wv_ref, ak_ref, yg, wqt, vt_s, s_scr, mx_scr, part, rbuf, patt, satt, gob, attt, wo_s, wg_s, wu_s, wd_s, n2_s, dn_s, *sems):
    chips, rows, mem, dim, hc, c, ff = dims
    QT = 2 * rows
    T = 2 * mem
    MC = min(256, mem)
    hh = hc // 2
    inner = hc * 64
    HR = hh * 64
    ring = Ring(chips)
    z, core, far = ring.z, ring.core, ring.far
    sub = rows // 2
    part_ = functools.partial
    xs, xr, ls = sems[14:]
    rsrc = lambda ref: (lambda half: ref.at[pl.ds(half * sub, sub)])
    y_g = Rows(ring, yg, rsrc(y_ref), sems[:6])
    go_g = Rows(ring, gog, rsrc(gob), sems[6:12])

    def merge(dst, src):
        for hl in range(hh):
            mr = slice(HR + hl, HR + hl + 1)
            lr = slice(HR + 8 + hl, HR + 9 + hl)
            m1, m2 = dst[mr, :], src[mr, :]
            m = jnp.maximum(m1, m2)
            a = jnp.exp2((m1 - m) * c)
            b = jnp.exp2((m2 - m) * c)
            rr = slice(hl * 64, (hl + 1) * 64)
            dst[rr, :] = dst[rr, :] * a + src[rr, :] * b
            dst[mr, :] = m
            dst[lr, :] = dst[lr, :] * a + src[lr, :] * b

    o_r = Reduce(ring, part, rbuf, merge, sems[12:14])
    loads = [pltpu.make_async_copy(src, dst, ls.at[7 + n]) for n, (src, dst) in enumerate((
        (wk_hbm, wk_ref), (wv_hbm, wv_ref), (wq_hbm, wq_ref), (wo_hbm, wo_s), (wg_hbm, wg_s), (wu_hbm, wu_s), (wd_hbm, wd_s)))]
    stores = [pltpu.make_async_copy(src, dst, ls.at[n]) for n, (src, dst) in enumerate(((k_s, k_out), (v_s, v_out), (kt_s, kt_out), (mg, mg_out), (qz, qz_out)))]
    for cp in loads[:3]:
        cp.start()
    ring.enter()
    y_g.start()
    mx_copy = remote(m_ref, mg, xs.at[0], xr.at[0], ring.partner)
    mx_copy.start()
    for cp in loads[3:]:
        cp.start()
    gob[...] = go_ref[...].astype(BF16)
    for half in range(2):
        yg[z, core, half] = y_ref[half * sub:(half + 1) * sub, :]
    hcol = pl.ds(pl.multiple_of(core * inner, 128), inner)
    qz[...] = jnp.zeros_like(qz)
    mask_lanes(ak_ref, len_ref, z * T)
    for cp in loads[:3]:
        cp.wait()
    wqt[...] = wq_ref[:, hcol].T
    wk = wk_ref[:, hcol]
    wv = wv_ref[:, hcol]

    moves = {"y": y_g, "go": go_g, "o": o_r}

    def acts(*point):
        return [go_g.start if e[1] == "start" else part_(moves[e[0]].move, *e[1:]) for e in FWD_PLAN.get(point, [])]

    def run(*point):
        for fn in acts(*point):
            fn()

    def project(src, base, blocks):
        for j in blocks:
            r = pl.ds(pl.multiple_of(base + j * MC, MC), MC)
            blk = src[j * MC:(j + 1) * MC, :]
            kb = mm(blk, wk).astype(BF16)
            vb = mm(blk, wv).astype(BF16)
            k_s[r, :] = kb
            v_s[r, :] = vb
            kt_s[:, r] = kb.T
            vt_s[:, r] = vb.T

    nb = mem // MC
    project(m_ref, core * mem, range(nb))
    run("s", 0)
    mx_copy.wait_recv()
    project(mg, (1 - core) * mem, range(nb // 2))
    run("s", 1)
    project(mg, (1 - core) * mem, range(nb // 2, nb))
    run("s", 2)
    for cp in stores[:4]:
        cp.start()
    gain = g_ref[0:1, :].astype(F32)
    one_row = jnp.where(lax.broadcasted_iota(jnp.int32, (16, QT), 0) == 0, 1.0, 0.0).astype(BF16)

    def lanes(chip):
        return pl.ds(pl.multiple_of(chip * QT, QT), QT)

    def prep(chip):
        n1 = rms_norm(yg[chip].reshape(QT, dim).astype(F32), gain).astype(BF16)
        qt = mm_bt(wqt[...], n1).astype(BF16)
        for h in range(hc):
            lo = h * 128 + (h % 2) * 64
            qz[lo:lo + 64, lanes(chip)] = qt[h * 64:(h + 1) * 64]

    def step(new, slot, old, pslot):
        if new is not None:
            chip, h = new
            rhs = jnp.concatenate([qz[pl.ds(pl.multiple_of(h * 128, 128), 128), lanes(chip)], one_row], axis=0)
            pair = pl.ds(pl.multiple_of((h // 2) * 128, 128), 128)
            mx = None
        if old is not None:
            ochip, half, hl = old
            m = jnp.max(mx_scr[pslot], axis=0, keepdims=True)
            vrow = pl.ds(pl.multiple_of((half * hh + hl) * 64, 64), 64)
            ls_ = None
            acc = None
        for j in range(T // MC):
            r = slice(j * MC, (j + 1) * MC)
            if new is not None:
                s = mm(jnp.concatenate([k_s[r, pair], ak_ref[r, 0:16]], axis=1), rhs)
                s_scr[slot, r, :] = s
                t = jnp.max(s.reshape(MC // 8, 8, QT), axis=0)
                mx = t if mx is None else jnp.maximum(mx, t)
            if old is not None:
                pr = jnp.exp2((s_scr[pslot, r, :] - m) * c)
                t = jnp.sum(pr.reshape(MC // 8, 8, QT), axis=0)
                ls_ = t if ls_ is None else ls_ + t
                dd = mm(vt_s[vrow, r], pr.astype(BF16))
                acc = dd if acc is None else acc + dd
        if new is not None:
            mx_scr[slot] = mx
        if old is not None:
            part[ochip, half, hl * 64:(hl + 1) * 64, :] = acc
            part[ochip, half, HR + hl:HR + hl + 1, :] = m
            part[ochip, half, HR + 8 + hl:HR + 9 + hl, :] = jnp.sum(ls_, axis=0, keepdims=True)

    offs = [o for o, _ in FWD_ORDER]
    halves = [h for _, h in FWD_ORDER]
    n = len(offs)
    fresh = [int(k + 1 < n and offs[k + 1] not in offs[:k + 1]) for k in range(n)]
    run("s", 3)
    y_g.ready(0)
    prep(z)
    step((z, halves[0] * hh), 0, None, None)

    def body(pair, carry):
        for u in range(2):
            i = 2 * pair + u
            i2 = jnp.minimum(i + 1, n - 1)
            chip, half = ring.chip(pick(i, offs)), pick(i, halves)
            chip2, half2 = ring.chip(pick(i2, offs)), pick(i2, halves)
            for k in range(hh):
                slot = (u * hh + k) % 2
                if k == hh - 1:
                    dispatch(pair, {kk // 2: acts("r", kk) + [part_(y_g.ready, offs[kk + 1])] for kk in range(u, n, 2) if fresh[kk]})
                    if any(fresh[u::2]):
                        pl.when(pick(i, fresh) == 1)(part_(prep, chip2))
                    new = (chip2, half2 * hh)
                else:
                    new = (chip, half * hh + k + 1)
                step(new, 1 - slot, (chip, half, k), slot)
                dispatch(pair, {kk // 2: acts("b", kk * hh + k) for kk in range(u, n, 2) if acts("b", kk * hh + k)})
        return carry

    gl = [pltpu.make_async_copy(gob.at[pl.ds(half * sub, sub)], gog.at[z, core, half], ls.at[5 + half]) for half in range(2)]
    for cp in gl:
        cp.start()
    lax.fori_loop(0, n // 2, body, 0)
    yc = pltpu.make_async_copy(yg, yall, ls.at[14])
    yc.start()
    stores[4].start()
    run("t", 0)
    run("t", 1)
    qmine = pl.ds(pl.multiple_of(core * rows, rows), rows)
    qother = pl.ds(pl.multiple_of((1 - core) * rows, rows), rows)
    for h in range(hc):
        half, hl = h // hh, h % hh
        m = part[z, half, HR + hl:HR + hl + 1, :]
        l = part[z, half, HR + 8 + hl:HR + 9 + hl, :]
        own[h * 64:(h + 1) * 64, :] = part[z, half, hl * 64:(hl + 1) * 64, :] / l
        own[inner + h:inner + h + 1, :] = m + jnp.log2(l) / c
    satt[...] = own[:inner, qother].astype(BF16)
    xo = remote(satt, patt, xs.at[1], xr.at[1], ring.partner)
    xo.start()
    attt[pl.ds(pl.multiple_of(core * inner, inner), inner), :] = own[:inner, qmine].astype(BF16)
    for cp in loads[3:]:
        cp.wait()
    run("t", 2)
    xo.wait()
    attt[pl.ds(pl.multiple_of((1 - core) * inner, inner), inner), :] = patt[...]

    att = attt[...].T
    att_ref[...] = att
    gain2 = g_ref[1:2, :].astype(F32)
    run("t", 3)
    hid = (y_ref[...].astype(F32) + mm(att, wo_s[...])).astype(BF16).astype(F32)
    inv = lax.rsqrt(jnp.mean(hid * hid, axis=-1, keepdims=True) + 1e-6)
    hhat = hid * inv
    n2 = (hhat * gain2).astype(BF16)
    fb = ff // 4
    n2_s[...] = n2
    dn_s[...] = jnp.zeros_like(dn_s)

    def mlp(f, carry):
        cols = pl.ds(pl.multiple_of(f * fb, fb), fb)
        wg, wu = wg_s[:, cols], wu_s[:, cols]
        g = mm(n2_s[...], wg)
        u = mm(n2_s[...], wu)
        ga = mm_bt(gob[...], wd_s[cols, :])
        sig = jax.nn.sigmoid(g)
        si = g * sig
        dn_s[...] += mm_bt((ga * u * (sig + si * (1.0 - sig))).astype(BF16), wg) + mm_bt((ga * si).astype(BF16), wu)
        dispatch(f, {n: acts("t", 4 + n) for n in range(4) if acts("t", 4 + n)})
        return carry

    lax.fori_loop(0, 4, mlp, 0)
    dn = dn_s[...]
    gsum = jnp.sum(dn * hhat, axis=0, keepdims=True)
    gn_ref[...] = jnp.zeros_like(gn_ref)
    for k in range(dim // QT):
        gn_ref[k:k + 1, :] = gsum[:, k * QT:(k + 1) * QT]
    t = dn * gain2
    gh = go_ref[...] + inv * (t - hhat * jnp.mean(t * hhat, axis=-1, keepdims=True))
    gh_ref[...] = gh
    dh_ref[...] = gh.astype(BF16)
    run("t", 8)
    for off in range(-far + 1, far + 1):
        go_g.ready(off)
    mx_copy.wait_send()
    for cp in [yc] + gl + stores:
        cp.wait()
    for obj in (y_g, go_g, o_r):
        obj.drain()


def fwd_call(dims, *args):
    chips, rows, mem, dim, hc, c, ff = dims
    hh = hc // 2
    inner = hc * 64
    QT = 2 * rows
    T = 2 * mem
    HR = hh * 64
    h2 = chips // 2
    v = pl.BlockSpec(memory_space=VMEM)
    hbm = pl.BlockSpec(memory_space=pl.ANY)
    S = jax.ShapeDtypeStruct
    s3 = (2, 2, h2)
    gshape = (chips, 2, 2, rows // 2, dim)
    rows_sems = [DMA((1,)), DMA(s3)] * 2 + [DMA((1,)), DMA((2,))]
    return pl.pallas_call(
        functools.partial(fwd_kernel, dims),
        out_shape=(S((inner + 8, QT), F32), S((rows, 2 * inner), BF16), S((rows, dim), BF16), S((rows, dim), F32), S((8, QT), F32),
                   S((T, inner), BF16), S((T, inner), BF16), S((inner, T), BF16), S((hc * 128, chips * QT), BF16), S((mem, dim), BF16), S(gshape, BF16), S(gshape, BF16)),
        in_specs=[pl.BlockSpec(memory_space=pltpu.SMEM)] + [v] * 4 + [hbm] * 7, out_specs=(v,) * 5 + (hbm,) * 7,
        scratch_shapes=[
            VMEM((T, inner), BF16), VMEM((T, inner), BF16), VMEM((inner, T), BF16), VMEM((hc * 128, chips * QT), BF16), VMEM((mem, dim), BF16),
            VMEM((dim, 2 * inner), BF16), VMEM((dim, 2 * inner), BF16), VMEM((dim, 2 * inner), BF16), VMEM((T, 128), BF16),
            VMEM(gshape, BF16), VMEM((inner, dim), BF16), VMEM((inner, T), BF16), VMEM((2, T, QT), F32), VMEM((2, 8, QT), F32),
            VMEM((chips, 2, HR + 16, QT), F32), VMEM((2, 2, h2, HR + 16, QT), F32), VMEM((inner, rows), BF16), VMEM((inner, rows), BF16),
            VMEM((rows, dim), BF16), VMEM((2 * inner, rows), BF16), VMEM((2 * inner, dim), BF16), VMEM((dim, ff), BF16), VMEM((dim, ff), BF16), VMEM((ff, dim), BF16), VMEM((rows, dim), BF16), VMEM((rows, dim), F32)]
        + rows_sems * 2 + [DMA((1,)), DMA(s3)] + [DMA((2,))] * 2 + [DMA((15,))],
        compiler_params=pltpu.CompilerParams(vmem_limit_bytes=62 * 1024 * 1024, collective_id=0, has_side_effects=True),
        cost_estimate=pl.CostEstimate(flops=10**10, bytes_accessed=30 << 20, transcendentals=0),
        name="attn_fwd")(*args)


def solution(mesh):
    group = mesh.shape['seq']
    row_spec = P(('data', 'seq'), None)
    part_vec = P('data')
    part_mat = P('data', None)
    part_cube = P('data', None, None)

    def device_step(dec_in, memory, mem_len, grad_out, norm_attn, wq, wk, wv, wo, norm_mlp, w_gate, w_up, w_down):
        rows, dim = dec_in.shape
        mem = memory.shape[0]
        heads, hd = wq.shape[1], wq.shape[2]
        inner = heads * hd
        chips = group // 2
        hc = heads // 2
        c = LOG2E * hd ** -0.5
        dims = (chips, rows, mem, dim, hc, c, w_gate.shape[1])
        wq2, wk2, wv2 = (w.reshape(dim, inner) for w in (wq, wk, wv))
        wo2 = wo.reshape(inner, dim)
        gains = jnp.stack([norm_attn, norm_mlp])

        own, attended, dh, grad_hidden, gn, k_c, v_c, kt_c, qz, mem_p, y_all, go_all = fwd_call(
            dims, mem_len, dec_in, grad_out, memory, gains, wq2, wk2, wv2, wo2, w_gate, w_up, w_down)
        gvec, dq_own, g_mem, g_wk, g_wv, g_wq, g_wo, g_down, g_gate, g_up, _ = bwd_call(
            dims, mem_len, dh, own, gn, attended, gains,
            k_c, v_c, kt_c, qz, wo2, wq2, wk2, wv2, memory, mem_p, y_all, go_all, w_gate, w_up, w_down)
        x_in = dec_in.astype(F32)
        _, norm_pull = jax.vjp(rms_norm, x_in, norm_attn.astype(F32))
        grad_x_norm, _ = norm_pull(mm_bt(dq_own.T, wq2))
        g_dec = grad_hidden + grad_x_norm
        cube = (dim, heads, hd)
        g_wq, g_wk, g_wv = (g.reshape(inner, dim).T.reshape(cube) for g in (g_wq, g_wk, g_wv))
        return (g_dec, g_mem, gvec[0], g_wq, g_wk, g_wv, g_wo.reshape(heads, hd, dim), gvec[1], g_gate, g_up, g_down)

    return jax.shard_map(device_step, mesh=mesh,
                         in_specs=(row_spec, row_spec, part_vec, row_spec) + (P(),) * 9,
                         out_specs=(row_spec, row_spec, part_vec, part_cube, part_cube, part_cube, part_cube, part_vec, part_mat, part_mat, part_mat),
                         check_vma=False)
```

profile of v0, /device:TPU:21, one launch (start us, length us, event | category | flops | bytes accessed | tf_op | source)
XLA Modules:
  0.0 283.3 jit_solution(8900566940740466348)
XLA Ops:
  0.7 2.5 copy.27.wq_hbm
  3.2 1.5 copy.28.wk_hbm
  4.7 1.4 copy.29.wv_hbm
  6.1 0.6 pad_maximum_fusion.g_ref
  7.4 86.7 %attn_fwd.1 = (f32[392,256]{1,0:T(8,128)}, bf16[128,768]{1,0:T(8,128)(2,1)}, bf16[128,768]{1,0:T(8,128)(2,1)}, f32[128,768]{1,0:T(8,128)}, f32[8,256]{1,0:T(8,12...) custom-call(s32[1]{0:T(128)S(6)} %copy.41.len_ref, ...), custom_call_target="tpu_custom_call" | custom-call | flops 10000000000 | bytes 31457280 | tf_op jit(solution)/shard_map/attn_fwd/pallas_call | solution.py:1022
  94.1 162.4 %attn_bwd.1 = (f32[2,768]{1,0:T(2,128)}, bf16[768,128]{1,0:T(8,128)(2,1)}, f32[1024,768]{1,0:T(8,128)}, f32[2,3,4,2,16,768]{5,4,3,2,1,0:T(8,128)}, f32[2,3,4,2,1...) custom-call(s32[1]{0:T(128)S(6)} %copy.41.len_ref, ...), custom_call_target="tpu_custom_call" | custom-call | flops 10000000000 | bytes 31457280 | tf_op jit(solution)/shard_map/attn_bwd/pallas_call | solution.py:757
  256.5 1.9 fusion
  258.5 1.9 fusion.2
  260.4 0.6 slice_reduce_fusion
  261.1 1.7 copy.42
  262.7 1.1 copy-done.4
  263.9 1.4 copy.43
  265.3 1.1 copy-done.3
  266.4 1.4 copy.44
  267.8 1.4 copy.45
  269.2 1.8 copy-done.1
  271.0 1.4 copy.46
  272.4 0.0 slice-start
  272.4 3.2 %copy.47 = f32[768,2048]{1,0:T(8,128)} copy(f32[768,2048]{1,0:T(8,128)S(1)} %bitcast.25) | data formatting | bytes 12582912
  275.6 0.1 slice-done.2
  275.7 1.3 slice-done.3
  277.0 2.9 %copy.48 = f32[768,2048]{1,0:T(8,128)} copy(f32[768,2048]{1,0:T(8,128)S(1)} %bitcast.23) | data formatting | bytes 12582912
  279.9 0.7 slice-done.1
  280.6 2.7 copy.49
  (32 shorter events, 0.1 us)
Async XLA Ops:
  0.6 2.5 copy-start.5
  0.7 4.0 %copy-start.6 = (bf16[768,12,64]{0,2,1:T(8,128)(2,1)S(1)}, bf16[768,12,64]{0,2,1:T(8,128)(2,1)}, u32[]{:S(2)}) copy-start(bf16[768,12,64]{0,2,1:T(8,128)(2,1)} %param.20) | copy-start | bytes 3538948
  3.2 2.9 %copy-start.9 = (bf16[768]{0:T(1024)(128)(2,1)S(1)}, bf16[768]{0:T(1024)(128)(2,1)}, u32[]{:S(2)}) copy-start(bf16[768]{0:T(1024)(128)(2,1)} %param.22) | copy-start | bytes 4612
  3.2 2.9 %copy-start.7 = (bf16[768]{0:T(1024)(128)(2,1)S(1)}, bf16[768]{0:T(1024)(128)(2,1)}, u32[]{:S(2)}) copy-start(bf16[768]{0:T(1024)(128)(2,1)} %param.17) | copy-start | bytes 4612
  256.5 3.9 %copy-start.8 = (f32[2,768]{1,0:T(2,128)S(1)}, f32[2,768]{1,0:T(2,128)}, u32[]{:S(2)}) copy-start(f32[2,768]{1,0:T(2,128)} %get-tuple-element.47) | copy-start | bytes 18436
  256.5 4.5 %copy-start = (f32[1024,768]{1,0:T(8,128)S(1)}, f32[1024,768]{1,0:T(8,128)}, u32[]{:S(2)}) copy-start(f32[1024,768]{1,0:T(8,128)} %get-tuple-element.74) | copy-start | bytes 9437188
  261.1 2.8 copy-start.4
  263.9 2.5 copy-start.3
  263.9 3.9 %copy-start.2 = (f32[2,3,4,2,16,768]{5,4,3,2,1,0:T(8,128)S(1)}, f32[2,3,4,2,16,768]{5,4,3,2,1,0:T(8,128)}, u32[]{:S(2)}) copy-start(f32[2,3,4,2,16,768]{5,4,3,2,1,0:T(8,128)} %get-tuple-element.50) | copy-start | bytes 7077892
  266.4 6.0 %slice-start.4 = ((s8[6291456]{0:T(1024)(128)(4,1)}), s8[4194304]{0:T(1024)(128)(4,1)S(1)}, s32[]{:S(2)}) async-start(s8[6291456]{0:T(1024)(128)(4,1)} %bitcast.24), calls=%async_computation.4 | async-start | bytes 8388608
  267.8 3.2 %copy-start.1 = (f32[768,768]{1,0:T(8,128)S(1)}, f32[768,768]{1,0:T(8,128)}, u32[]{:S(2)}) copy-start(f32[768,768]{1,0:T(8,128)} %get-tuple-element.51) | copy-start | bytes 7077892
  267.8 4.6 %slice-start.5 = ((s8[6291456]{0:T(1024)(128)(4,1)}), s8[2097152]{0:T(1024)(128)(4,1)S(1)}, s32[]{:S(2)}) async-start(s8[6291456]{0:T(1024)(128)(4,1)} %bitcast.24), calls=%async_computation.5 | async-start | bytes 4194304
  270.9 4.7 %slice-start.2 = ((s8[6291456]{0:T(1024)(128)(4,1)}), s8[4194304]{0:T(1024)(128)(4,1)S(1)}, s32[]{:S(2)}) async-start(s8[6291456]{0:T(1024)(128)(4,1)} %bitcast.22), calls=%async_computation.2 | async-start | bytes 8388608
  272.4 4.6 %slice-start.3 = ((s8[6291456]{0:T(1024)(128)(4,1)}), s8[2097152]{0:T(1024)(128)(4,1)S(1)}, s32[]{:S(2)}) async-start(s8[6291456]{0:T(1024)(128)(4,1)} %bitcast.22), calls=%async_computation.3 | async-start | bytes 4194304
  272.4 7.5 %slice-start = ((s8[6291456]{0:T(1024)(128)(4,1)}), s8[4194304]{0:T(1024)(128)(4,1)S(1)}, s32[]{:S(2)}) async-start(s8[6291456]{0:T(1024)(128)(4,1)} %bitcast.20), calls=%async_computation | async-start | bytes 8388608
  277.0 3.6 %slice-start.1 = ((s8[6291456]{0:T(1024)(128)(4,1)}), s8[2097152]{0:T(1024)(128)(4,1)S(1)}, s32[]{:S(2)}) async-start(s8[6291456]{0:T(1024)(128)(4,1)} %bitcast.20), calls=%async_computation.1 | async-start | bytes 4194304
where the time goes:
time: 284 us; the launch traced here: 283 us
  Pallas kernels  249 us (88%)
  local copies, waits for them, and re-layouts  28.3 us (10%)
    pallas_call x1, Pallas kernels, bwd_call(): pl.pallas_call(functools.partial(bwd_kernel, dims), out_shape=(S((2, dim)...  162 us
    pallas_call x1, Pallas kernels, fwd_call(): pl.pallas_call(functools.partial(fwd_kernel, dims), out_shape=(S((inner +...  86.7 us
    unnamed x40, local copies, waits for them, and re-layouts  22.3 us

commit v1 on v0

--- a/solution.py
+++ b/solution.py
@@ -73,7 +73,8 @@
 }
 BWD_PLAN = {
     ("b", 1): [("dh", 0, 0, 1), ("dh", 1, 1, 1)],
-    ("b", 11): [("dh", 0, 1, 3), ("dh", 1, 0, 3), ("st", 0, 0, 3), ("st", 1, 1, 3), ("st", 0, 1, 3), ("st", 1, 0, 3)],
+    ("b", 10): [("dh", 0, 1, 3), ("dh", 1, 0, 3), ("st", 0, 0, 3), ("st", 1, 1, 3)],
+    ("b", 11): [("st", 0, 1, 3), ("st", 1, 0, 3)],
     ("b", 12): [("dq0", 0, 0, 4)],
     ("b", 13): [("dq0", 1, 1, 4)],
     ("b", 14): [("att", 0, 0, 1), ("att", 1, 1, 1)],
@@ -82,73 +83,74 @@
     ("b", 17): [("dq0", 1, 1, 3)],
     ("b", 18): [("att", 0, 0, 2), ("att", 1, 1, 2)],
     ("b", 19): [("dq0", 0, 1, 2), ("att", 1, 0, 2)],
-    ("b", 2): [("dh", 0, 1, 1), ("dh", 1, 0, 1), ("st", 0, 0, 1), ("st", 1, 1, 1)],
+    ("b", 2): [("dh", 0, 1, 1), ("dh", 1, 0, 1), ("st", 0, 0, 1), ("st", 1, 1, 1), ("st", 0, 1, 1), ("st", 1, 0, 1)],
     ("b", 20): [("dq0", 1, 0, 2), ("att", 0, 1, 2)],
     ("b", 21): [("dq0", 0, 0, 2), ("dq0", 1, 1, 2)],
     ("b", 22): [("att", 0, 0, 3), ("att", 1, 1, 3)],
     ("b", 23): [("dq0", 0, 1, 1), ("ar0", 0, 1, 3), ("ar0", 1, 0, 3), ("ar0", 0, 0, 4), ("ar0", 1, 1, 4), ("att", 1, 0, 3)],
     ("b", 24): [("dq0", 1, 0, 1), ("dq1", 0, 0, 4), ("att", 0, 1, 3)],
     ("b", 25): [("dq0", 0, 0, 1), ("dq0", 1, 1, 1), ("dq1", 1, 1, 4)],
-    ("b", 27): [("dq1", 0, 1, 3), ("att", 0, 0, 4), ("att", 1, 1, 4)],
-    ("b", 28): [("dq0", 0, 1, 0), ("dq1", 1, 0, 3), ("ar0", 1, 0, 2), ("ar0", 1, 1, 3), ("ar0", 0, 1, 2)],
+    ("b", 26): [("att", 0, 0, 4), ("att", 1, 1, 4)],
+    ("b", 27): [("dq0", 0, 1, 0), ("dq1", 0, 1, 3), ("ar0", 1, 0, 2)],
+    ("b", 28): [("dq1", 1, 0, 3), ("ar0", 1, 1, 3), ("ar0", 0, 1, 2)],
     ("b", 29): [("dq0", 1, 0, 0), ("ar0", 0, 0, 3)],
-    ("b", 3): [("st", 0, 1, 1), ("st", 1, 0, 1)],
     ("b", 30): [("dq0", 1, 1, 0), ("dq1", 0, 0, 3)],
-    ("b", 31): [("dq0", 0, 0, 0), ("ds0", "start"), ("dq1", 1, 1, 3)],
-    ("b", 32): [("dq1", 0, 1, 2), ("dq1", 1, 0, 2)],
-    ("b", 33): [("ar0", 0, 1, 1), ("ar0", 1, 0, 1)],
-    ("b", 34): [("ar0", 0, 0, 2), ("ar0", 1, 1, 2), ("ds0", 1, 1, 1)],
-    ("b", 35): [("dq1", 0, 0, 2), ("dq1", 1, 1, 2), ("ar1", 0, 1, 3), ("ar1", 1, 0, 3), ("ar1", 0, 0, 4), ("ar1", 1, 1, 4), ("ds0", 1, 0, 1), ("ds0", 0, 0, 1), ("ds0", 0, 1, 1)],
-    ("b", 36): [("dq1", 0, 1, 1), ("dq1", 1, 0, 1), ("dq2", 0, 0, 4), ("ar0", 0, 1, 0), ("ar0", 1, 0, 0)],
-    ("b", 37): [("dq2", 1, 1, 4), ("ar0", 0, 0, 1), ("ar0", 1, 1, 1)],
-    ("b", 38): [("dq1", 0, 0, 1), ("ds0", 1, 1, 2)],
-    ("b", 39): [("dq1", 1, 1, 1), ("dq2", 0, 1, 3), ("ar1", 0, 1, 2)],
-    ("b", 40): [("dq2", 1, 0, 3), ("ar1", 1, 0, 2), ("ar1", 0, 0, 3), ("ar1", 1, 1, 3), ("ds0", 0, 0, 2)],
-    ("b", 41): [("ds0", 0, 1, 2), ("ds0", 1, 0, 2)],
-    ("b", 42): [("dq1", 0, 1, 0), ("dq1", 1, 0, 0)],
-    ("b", 43): [("dq2", 0, 0, 3), ("dq2", 1, 1, 3)],
-    ("b", 44): [("ar0", 0, 0, 0), ("ar0", 1, 1, 0), ("as0", "start"), ("ds0", 1, 1, 3)],
-    ("b", 45): [("dq1", 0, 0, 0), ("dq1", 1, 1, 0), ("ds1", "start")],
-    ("b", 46): [("dq2", 0, 1, 2), ("dq2", 1, 0, 2), ("ar1", 0, 1, 1)],
-    ("b", 47): [("ar1", 1, 0, 1), ("ar1", 0, 0, 2), ("ar1", 1, 1, 2), ("ar2", 0, 1, 3), ("ar2", 1, 0, 3), ("ar2", 0, 0, 4), ("ar2", 1, 1, 4), ("ds0", 0, 0, 3), ("ds0", 0, 1, 3), ("ds0", 1, 0, 3)],
+    ("b", 31): [("dq0", 0, 0, 0), ("ds0", "start"), ("dq1", 1, 1, 3), ("ar0", 1, 0, 1)],
+    ("b", 32): [("dq1", 0, 1, 2), ("dq1", 1, 0, 2), ("ar0", 0, 1, 1)],
+    ("b", 33): [("ar0", 0, 0, 2), ("ar0", 1, 1, 2)],
+    ("b", 34): [("dq1", 0, 0, 2), ("ds0", 1, 1, 1), ("ds0", 1, 0, 1)],
+    ("b", 35): [("dq1", 1, 1, 2), ("dq1", 0, 1, 1), ("ar0", 1, 0, 0), ("ar1", 0, 1, 3), ("ar1", 1, 0, 3), ("ar1", 0, 0, 4), ("ar1", 1, 1, 4), ("ds0", 0, 0, 1), ("ds0", 0, 1, 1)],
+    ("b", 36): [("dq1", 1, 0, 1), ("dq2", 0, 0, 4), ("ar0", 0, 1, 0), ("ar0", 0, 0, 1), ("ar0", 1, 1, 1)],
+    ("b", 37): [("dq1", 0, 0, 1), ("dq2", 1, 1, 4), ("ds0", 1, 1, 2), ("ds0", 1, 0, 2)],
+    ("b", 38): [("dq1", 0, 1, 0), ("dq1", 1, 1, 1)],
+    ("b", 39): [("dq2", 0, 1, 3), ("ar1", 0, 1, 2), ("ar1", 1, 0, 2)],
+    ("b", 40): [("dq2", 1, 0, 3), ("ar1", 0, 0, 3), ("ar1", 1, 1, 3), ("ds0", 0, 0, 2)],
+    ("b", 41): [("dq1", 1, 0, 0), ("ds0", 0, 1, 2)],
+    ("b", 42): [("dq2", 0, 0, 3), ("ar0", 1, 1, 0)],
+    ("b", 43): [("dq2", 1, 1, 3), ("ar0", 0, 0, 0), ("as0", "start"), ("ds0", 1, 1, 3), ("dq1", 0, 0, 0), ("ds0", 1, 0, 3)],
+    ("b", 45): [("dq1", 1, 1, 0), ("ds1", "start"), ("dq2", 0, 1, 2), ("ar1", 0, 1, 1), ("ar1", 1, 0, 1)],
+    ("b", 46): [("dq2", 1, 0, 2), ("ar1", 0, 0, 2), ("ds0", 0, 0, 3)],
+    ("b", 47): [("dq2", 0, 0, 2), ("dq2", 1, 1, 2), ("ar1", 1, 1, 2), ("ar2", 0, 1, 3), ("ar2", 1, 0, 3), ("ar2", 0, 0, 4), ("ar2", 1, 1, 4), ("ds0", 0, 1, 3)],
     ("b", 5): [("dh", 0, 0, 2), ("dh", 1, 1, 2)],
-    ("b", 7): [("dh", 0, 1, 2), ("dh", 1, 0, 2), ("st", 0, 0, 2), ("st", 1, 1, 2), ("st", 0, 1, 2), ("st", 1, 0, 2)],
+    ("b", 6): [("dh", 0, 1, 2), ("dh", 1, 0, 2), ("st", 0, 0, 2), ("st", 1, 1, 2)],
+    ("b", 7): [("st", 0, 1, 2), ("st", 1, 0, 2)],
     ("b", 9): [("dh", 0, 0, 3), ("dh", 1, 1, 3)],
-    ("f", 0): [("ar1", 1, 0, 0), ("ar1", 0, 0, 1), ("ar1", 1, 1, 1), ("ar2", 0, 1, 2)],
-    ("f", 11): [("dq2", 0, 1, 0), ("dq2", 1, 0, 0)],
-    ("f", 13): [("ar1", 0, 0, 0), ("ar1", 1, 1, 0), ("as1", "start")],
+    ("f", 1): [("dq2", 0, 0, 1), ("ar1", 1, 1, 1), ("ar2", 0, 1, 2), ("ar2", 1, 0, 2)],
+    ("f", 10): [("dq2", 1, 1, 0), ("ar1", 0, 0, 0)],
+    ("f", 12): [("dq2", 0, 0, 0), ("ds2", "start"), ("ar1", 1, 1, 0), ("as1", "start")],
     ("f", 14): [("ar2", 0, 1, 1), ("ar2", 1, 0, 1)],
     ("f", 16): [("ar2", 0, 0, 2), ("ar2", 1, 1, 2)],
-    ("f", 17): [("dq2", 0, 0, 0), ("dq2", 1, 1, 0), ("ds2", "start"), ("as0", 0, 0, 3), ("as0", 1, 1, 3)],
-    ("f", 18): [("as0", 0, 1, 3), ("as0", 1, 0, 3)],
-    ("f", 19): [("ds1", 0, 0, 3), ("ds1", 1, 1, 3)],
-    ("f", 2): [("ar2", 1, 0, 2), ("ar2", 0, 0, 3)],
-    ("f", 21): [("ds1", 0, 1, 3), ("ds1", 1, 0, 3)],
+    ("f", 17): [("as0", 0, 0, 3), ("as0", 1, 1, 3), ("as0", 0, 1, 3), ("as0", 1, 0, 3), ("ds1", 0, 0, 3), ("ds1", 1, 1, 3), ("ds1", 0, 1, 3), ("ds1", 1, 0, 3)],
+    ("f", 19): [("ds2", 0, 0, 1), ("ds2", 1, 1, 1)],
+    ("f", 21): [("ds2", 0, 1, 1), ("ds2", 1, 0, 1)],
     ("f", 23): [("as1", 0, 0, 1), ("as1", 1, 1, 1)],
     ("f", 25): [("as1", 0, 1, 1), ("as1", 1, 0, 1)],
-    ("f", 26): [("ar2", 0, 1, 0), ("ar2", 1, 0, 0), ("ar2", 0, 0, 1), ("ar2", 1, 1, 1), ("ds2", 0, 0, 1), ("ds2", 1, 1, 1), ("ds2", 0, 1, 1), ("ds2", 1, 0, 1)],
-    ("f", 28): [("as0", 0, 0, 4), ("as0", 1, 1, 4)],
-    ("f", 3): [("ar2", 1, 1, 3), ("ds0", 0, 0, 4)],
-    ("f", 30): [("ds1", 0, 0, 4), ("ds1", 1, 1, 4)],
+    ("f", 26): [("ar2", 0, 1, 0), ("ar2", 1, 0, 0), ("ar2", 0, 0, 1), ("ar2", 1, 1, 1), ("as0", 0, 0, 4), ("as0", 1, 1, 4), ("ds1", 0, 0, 4), ("ds1", 1, 1, 4)],
+    ("f", 28): [("ds2", 0, 0, 2), ("ds2", 1, 1, 2)],
+    ("f", 3): [("ar2", 0, 0, 3), ("ar2", 1, 1, 3)],
+    ("f", 30): [("ds2", 0, 1, 2), ("ds2", 1, 0, 2)],
     ("f", 32): [("as1", 0, 0, 2), ("as1", 1, 1, 2)],
     ("f", 34): [("as1", 0, 1, 2), ("as1", 1, 0, 2)],
-    ("f", 35): [("ar2", 0, 0, 0), ("ar2", 1, 1, 0), ("as2", "start"), ("ds2", 0, 0, 2), ("ds2", 1, 1, 2), ("ds2", 0, 1, 2), ("ds2", 1, 0, 2)],
-    ("f", 6): [("dq2", 0, 0, 1), ("dq2", 1, 1, 1)],
-    ("f", 8): [("as0", 0, 0, 2), ("as0", 1, 1, 2), ("as0", 0, 1, 2), ("as0", 1, 0, 2), ("ds1", 0, 0, 2), ("ds1", 1, 1, 2), ("ds1", 0, 1, 2), ("ds1", 1, 0, 2)],
-    ("h", 0): [("dq2", 0, 0, 2), ("dq2", 1, 1, 2)],
-    ("h", 1): [("as0", 0, 0, 1), ("as0", 1, 1, 1)],
-    ("h", 3): [("as0", 0, 1, 1), ("as0", 1, 0, 1), ("ds0", 1, 1, 4), ("ds1", 0, 0, 1)],
-    ("h", 4): [("ds1", 0, 1, 1), ("ds1", 1, 1, 1)],
-    ("h", 5): [("ds1", 1, 0, 1)],
-    ("h", 6): [("dq2", 0, 1, 1)],
-    ("h", 7): [("dq2", 1, 0, 1), ("ar1", 0, 1, 0)],
-    ("m", 0): [("as1", 0, 0, 3), ("as1", 1, 1, 3), ("as1", 0, 1, 3), ("as1", 1, 0, 3)],
-    ("m", 2): [("as2", 0, 0, 1), ("as2", 1, 1, 1)],
-    ("m", 3): [("as2", 0, 1, 1), ("as2", 1, 0, 1)],
-    ("m", 4): [("ds2", 0, 0, 3), ("ds2", 1, 1, 3), ("ds2", 0, 1, 3), ("ds2", 1, 0, 3), ("ds2", 0, 0, 4), ("ds2", 1, 1, 4)],
-    ("q", 0): [("as1", 0, 0, 4), ("as1", 1, 1, 4), ("as2", 0, 0, 2), ("as2", 1, 1, 2), ("as2", 0, 1, 2), ("as2", 1, 0, 2)],
-    ("q", 6): [("as2", 0, 0, 3), ("as2", 1, 1, 3)],
-    ("q", 8): [("as2", 0, 1, 3), ("as2", 1, 0, 3), ("as2", 0, 0, 4), ("as2", 1, 1, 4)],
+    ("f", 35): [("ar2", 0, 0, 0), ("ar2", 1, 1, 0), ("as2", "start"), ("ds2", 0, 0, 3), ("as1", 0, 0, 3), ("ds2", 1, 1, 3), ("as1", 1, 1, 3), ("ds2", 0, 1, 3), ("ds2", 1, 0, 3)],
+    ("f", 5): [("as0", 0, 0, 2), ("as0", 1, 1, 2)],
+    ("f", 7): [("as0", 0, 1, 2), ("as0", 1, 0, 2)],
+    ("f", 8): [("dq2", 0, 1, 0), ("dq2", 1, 0, 0), ("ds1", 0, 0, 2), ("ds1", 1, 1, 2), ("ds1", 0, 1, 2), ("ds1", 1, 0, 2)],
+    ("h", 0): [("as0", 0, 0, 1), ("as0", 1, 1, 1)],
+    ("h", 1): [("as0", 0, 1, 1), ("as0", 1, 0, 1), ("ds1", 0, 0, 1), ("ds0", 1, 1, 4)],
+    ("h", 2): [("ds1", 0, 1, 1), ("ds1", 1, 1, 1)],
+    ("h", 3): [("ds1", 1, 0, 1)],
+    ("h", 4): [("dq2", 0, 1, 1), ("ar1", 1, 0, 0)],
+    ("h", 5): [("ar1", 0, 1, 0), ("dq2", 1, 0, 1)],
+    ("h", 6): [("ar1", 0, 0, 1), ("ds0", 0, 0, 4)],
+    ("h", 7): [("dq2", 1, 1, 1)],
+    ("m", 1): [("as1", 0, 1, 3), ("as1", 1, 0, 3)],
+    ("m", 3): [("as2", 0, 0, 1), ("as2", 1, 1, 1)],
+    ("m", 4): [("ds2", 0, 0, 4), ("ds2", 1, 1, 4)],
+    ("q", 0): [("as2", 0, 1, 1), ("as2", 1, 0, 1)],
+    ("q", 1): [("as1", 0, 0, 4), ("as1", 1, 1, 4)],
+    ("q", 3): [("as2", 0, 0, 2), ("as2", 1, 1, 2)],
+    ("q", 6): [("as2", 0, 1, 2), ("as2", 1, 0, 2)],
+    ("q", 8): [("as2", 0, 0, 3), ("as2", 1, 1, 3), ("as2", 0, 1, 3), ("as2", 1, 0, 3), ("as2", 0, 0, 4), ("as2", 1, 1, 4)],
     ("r", 12): [("dh", 0, 0, 4), ("dh", 1, 1, 4), ("att", "start"), ("st", 0, 0, 4), ("st", 1, 1, 4)],
 }
 
@@ -329,10 +331,10 @@
     return hi, mid, lo
 
 
-def bwd_kernel(dims, len_ref, dh_ref, own_ref, gn_ref, att_ref, g_ref,
+def bwd_kernel(dims, len_ref, dh_ref, own_ref, gn_ref, att_ref, y_ref, gh_ref, g_ref,
                k_hbm, v_hbm, kt_hbm, qz_hbm, wo_hbm, wq_hbm, wk_hbm, wv_hbm, ma_hbm, mb_hbm, y_hbm, gog, wg_hbm, wu_hbm, wd_hbm,
-               gvec_ref, dqo_ref, gmem, gwk, gwv, gwq, gwo, gdown, ggate, gup, attg,
-               k_ref, v_ref, kt_ref, qz_ref, wo_ref, wq_ref, wk_ref, wv_ref, ak_ref,
+               gvec_ref, gdec_ref, gmem, gwk, gwv, gwq, gwo, gdown, ggate, gup, attg,
+               dqo_ref, k_ref, v_ref, kt_ref, qz_ref, wo_ref, wq_ref, wk_ref, wv_ref, ak_ref,
                dhg, doz, aqs, ads, stb, dk, dv, dkv, dkvp, dqp, dqr, dqa, arp, arr, ara, pvec, pdq, spb,
                msc, ybuf, abuf, wbuf, dbuf, wt, gst, gsw, gwo_s, gwq_s,
                *sems):
@@ -578,8 +580,8 @@
 
     def w_fetch(f, slot):
         cols = pl.ds(pl.multiple_of(core * fh + f * FT, FT), FT)
-        return (pltpu.make_async_copy(wg_hbm.at[:, cols], wbuf.at[slot, 0], wsem.at[slot, 0]),
-                pltpu.make_async_copy(wu_hbm.at[:, cols], wbuf.at[slot, 1], wsem.at[slot, 1]),
+        return (pltpu.make_async_copy(wg_hbm.at[:, cols], wbuf.at[0], wsem.at[slot, 0]),
+                pltpu.make_async_copy(wu_hbm.at[:, cols], wbuf.at[1], wsem.at[slot, 1]),
                 pltpu.make_async_copy(wd_hbm.at[cols], dbuf.at[slot], wsem.at[slot, 2]))
 
     for cp in w_fetch(0, 0):
@@ -589,50 +591,52 @@
 
     def block(f, n):
         if n == 0:
-            return partner_block(gst.at[0, pl.ds(0, FT)], gdown.at[pl.ds(pl.multiple_of(core * fh + f * FT, FT), FT)], f)
-        return partner_block(gsw.at[n - 1], (ggate, gup)[n - 1].at[:, pl.ds(pl.multiple_of(core * fh + f * FT, FT), FT)], n * nf + f)
+            return partner_block(gst.at[f % 2, pl.ds(0, FT)], gdown.at[pl.ds(pl.multiple_of(core * fh + f * FT, FT), FT)], f)
+        return partner_block(gsw.at[f % 2, n - 1], (ggate, gup)[n - 1].at[:, pl.ds(pl.multiple_of(core * fh + f * FT, FT), FT)], n * nf + f)
 
     def mlp(f, carry):
         slot = f % 2
         for cp in w_fetch(f, slot):
             cp.wait()
 
+        for n in range(2):
+            wt[n] = wbuf[n].T
+
         @pl.when(f + 1 < nf)
         def _():
             for cp in w_fetch(f + 1, 1 - slot):
                 cp.start()
-        for n in range(2):
-            wt[n] = wbuf[slot, n].T
-
-        def act_chunk(ch, cc):
-            q = lanes(ch)
-            n2t = qz_ref[0:dim, q]
-            g = mm(wt[0], n2t)
-            u = mm(wt[1], n2t)
-            ga = mm_bt(dbuf[slot], dhg[ch].reshape(QT, dim))
-            sig = jax.nn.sigmoid(g)
-            si = g * sig
-            doz[0:FT, q] = (si * u).astype(BF16)
-            doz[FT:2 * FT, q] = (ga * u * (sig + si * (1.0 - sig))).astype(BF16)
-            doz[2 * FT:3 * FT, q] = (ga * si).astype(BF16)
-            dispatch(f * 9 + ch, f_table)
+
+        def act_pair(k, cc):
+            for ch in (2 * k, 2 * k + 1):
+                q = lanes(ch)
+                n2t = qz_ref[0:dim, q]
+                g = mm(wt[0], n2t)
+                u = mm(wt[1], n2t)
+                ga = mm_bt(dbuf[slot], dhg[ch].reshape(QT, dim))
+                sig = jax.nn.sigmoid(g)
+                si = g * sig
+                doz[0:FT, q] = (si * u).astype(BF16)
+                doz[FT:2 * FT, q] = (ga * u * (sig + si * (1.0 - sig))).astype(BF16)
+                doz[2 * FT:3 * FT, q] = (ga * si).astype(BF16)
+            dispatch(f * 9 + 2 * k + 1, f_table)
             return cc
 
-        lax.fori_loop(0, chips, act_chunk, 0)
-
-        @pl.when(f > 0)
+        lax.fori_loop(0, chips // 2, act_pair, 0)
+
+        @pl.when(f > 1)
         def _():
             for n in range(3):
-                both_wait(block(f - 1, n))
+                both_wait(block(f - 2, n))
         acc = [None] * 3
         for ch in range(chips):
             q = slice(ch * QT, (ch + 1) * QT)
             n2t = qz_ref[0:dim, q]
             for n, d in enumerate((mm(doz[0:FT, q], dhg[ch].reshape(QT, dim)), mm_bt(n2t, doz[FT:2 * FT, q]), mm_bt(n2t, doz[2 * FT:3 * FT, q]))):
                 acc[n] = d if acc[n] is None else acc[n] + d
-        gst[0, 0:FT] = acc[0]
-        gsw[0] = acc[1]
-        gsw[1] = acc[2]
+        gst[slot, 0:FT] = acc[0]
+        gsw[slot, 0] = acc[1]
+        gsw[slot, 1] = acc[2]
         for n in range(3):
             both_start(block(f, n))
         dispatch(f * 9 + 8, f_table)
@@ -643,8 +647,9 @@
         remote(dkvp.at[p], dkvp.at[p], xs.at[p], xr.at[p], ring.partner).wait_recv()
     nb = 4
     w = mem // nb
-    for n in range(3):
-        both_wait(block(nf - 1, n))
+    for f in (nf - 2, nf - 1):
+        for n in range(3):
+            both_wait(block(f, n))
 
     def gm(b):
         return pltpu.make_async_copy(gst.at[b % 2, pl.ds(0, w)], gmem.at[pl.ds(pl.multiple_of(b * w, w), w)], gl.at[3 * nf + 2 + b % 2])
@@ -712,6 +717,11 @@
         dqo_ref[own_r, :] = dqa[p, z, :, :, qmine].reshape(128, rows)
         xq(p).wait()
         dqo_ref[oth_r, :] = pdq[p].reshape(128, rows)
+    x = y_ref[...].astype(F32)
+    inv = lax.rsqrt(jnp.mean(x * x, axis=-1, keepdims=True) + 1e-6)
+    xhat = x * inv
+    t = mm_bt(dqo_ref[...].T, wq_ref[...]) * gain
+    gdec_ref[...] = gh_ref[...] + inv * (t - xhat * jnp.mean(t * xhat, axis=-1, keepdims=True))
     run("q", chips)
     wkv_out = []
     for p in range(np_):
@@ -756,21 +766,21 @@
     wsq = VMEM((dim, 2 * inner), BF16)
     return pl.pallas_call(
         functools.partial(bwd_kernel, dims),
-        out_shape=(S((2, dim), F32), S((2 * inner, rows), BF16), S((mem, dim), F32), S((2, np_, chips // 2, 2, seg, dim), F32), S((2, np_, chips // 2, 2, seg, dim), F32), S((2 * inner, dim), F32), S((2 * inner, dim), F32),
+        out_shape=(S((2, dim), F32), S((rows, dim), F32), S((mem, dim), F32), S((2, np_, chips // 2, 2, seg, dim), F32), S((2, np_, chips // 2, 2, seg, dim), F32), S((2 * inner, dim), F32), S((2 * inner, dim), F32),
                    S((ff, dim), F32), S((dim, ff), F32), S((dim, ff), F32), S(gshape, BF16)),
-        in_specs=[pl.BlockSpec(memory_space=pltpu.SMEM)] + [v] * 5 + [hbm] * 15, out_specs=(v,) * 2 + (hbm,) * 9,
+        in_specs=[pl.BlockSpec(memory_space=pltpu.SMEM)] + [v] * 7 + [hbm] * 15, out_specs=(v,) * 2 + (hbm,) * 9,
         scratch_shapes=[
-            VMEM((T, inner), BF16), VMEM((T, inner), BF16), VMEM((inner, T), BF16), VMEM((hc * 128, cols), BF16), VMEM((2 * inner, dim), BF16), wsq, wsq, wsq, VMEM((T, 128), BF16),
+            VMEM((2 * inner, rows), BF16), VMEM((T, inner), BF16), VMEM((T, inner), BF16), VMEM((inner, T), BF16), VMEM((hc * 128, cols), BF16), VMEM((2 * inner, dim), BF16), wsq, wsq, wsq, VMEM((T, 128), BF16),
             VMEM(gshape, BF16), VMEM((max(hc * 128, 3 * FT), cols), BF16), VMEM((hc * 16, cols), BF16), VMEM((hc * 16, cols), BF16),
             VMEM((chips, 2, 8, QT), F32), VMEM((inner, T), F32), VMEM((inner, T), F32), VMEM((np_, 256, T), BF16), VMEM((np_, 256, mem), BF16),
             VMEM((np_, chips, 2, 64, QT), F32), VMEM((np_, 2, 2, h2, 64, QT), F32), VMEM((np_, chips, 2, 64, QT), BF16),
             VMEM((np_, chips, 2, seg, dim), F32), VMEM((np_, 2, 2, h2, seg, dim), F32), VMEM((np_, chips, 2, seg, dim), F32),
             VMEM((8, dim), F32), VMEM((np_, 2, 64, rows), BF16), VMEM((8, dim), F32),
             VMEM((2, mem, dim), BF16), VMEM((2, 2, 2, rows // 2, dim), BF16), VMEM((2, 2, 2, rows // 2, dim), BF16),
-            VMEM((2, 2, dim, FT), BF16), VMEM((2, FT, dim), BF16), VMEM((2, FT, dim), BF16), VMEM((2, max(FT, mem // 4), dim), F32), VMEM((2, dim, FT), F32),
+            VMEM((2, dim, FT), BF16), VMEM((2, FT, dim), BF16), VMEM((2, FT, dim), BF16), VMEM((2, max(FT, mem // 4), dim), F32), VMEM((2, 2, dim, FT), F32),
             VMEM((inner, dim), F32), VMEM((inner, dim), F32)]
         + rows_sems * 2 + two * (1 + 4 * np_) + [DMA((4 * np_ + 1,))] * 2 + [DMA((2 + 2 * np_,)), DMA((14,)), DMA((14,)), DMA((16,)), DMA((2, 3)), DMA((2, 2)), DMA((10,))],
-        compiler_params=pltpu.CompilerParams(vmem_limit_bytes=66_900_000, collective_id=1, has_side_effects=True),
+        compiler_params=pltpu.CompilerParams(vmem_limit_bytes=67_043_328, collective_id=1, has_side_effects=True),
         cost_estimate=pl.CostEstimate(flops=10**10, bytes_accessed=30 << 20, transcendentals=0),
         name="attn_bwd")(*args)
 
@@ -1058,13 +1068,9 @@
 
         own, attended, dh, grad_hidden, gn, k_c, v_c, kt_c, qz, mem_p, y_all, go_all = fwd_call(
             dims, mem_len, dec_in, grad_out, memory, gains, wq2, wk2, wv2, wo2, w_gate, w_up, w_down)
-        gvec, dq_own, g_mem, g_wk, g_wv, g_wq, g_wo, g_down, g_gate, g_up, _ = bwd_call(
-            dims, mem_len, dh, own, gn, attended, gains,
+        gvec, g_dec, g_mem, g_wk, g_wv, g_wq, g_wo, g_down, g_gate, g_up, _ = bwd_call(
+            dims, mem_len, dh, own, gn, attended, dec_in, grad_hidden, gains,
             k_c, v_c, kt_c, qz, wo2, wq2, wk2, wv2, memory, mem_p, y_all, go_all, w_gate, w_up, w_down)
-        x_in = dec_in.astype(F32)
-        _, norm_pull = jax.vjp(rms_norm, x_in, norm_attn.astype(F32))
-        grad_x_norm, _ = norm_pull(mm_bt(dq_own.T, wq2))
-        g_dec = grad_hidden + grad_x_norm
         cube = (dim, heads, hd)
         g_wq, g_wk, g_wv = (g.reshape(inner, dim).T.reshape(cube) for g in (g_wq, g_wk, g_wv))
         return (g_dec, g_mem, gvec[0], g_wq, g_wk, g_wv, g_wo.reshape(heads, hd, dim), gvec[1], g_gate, g_up, g_down)

time: 284 us -> 279 us (0.982)
  Pallas kernels: 249 us -> 243 us
  local copies, waits for them, and re-layouts: 28.3 us -> 33.2 us
    pallas_call x1, Pallas kernels: 162 us -> 156 us  [bwd_call(): pl.pallas_call(functools.partial(bwd_kernel, dims), out_shape=(S((2, dim)...]
    unnamed x40 -> x33, local copies, waits for them, and re-layouts: 22.3 us -> 25.1 us
where the time goes in v1:
time: 279 us; the launch traced here: 278 us
  Pallas kernels  243 us (87%)
  local copies, waits for them, and re-layouts  33.2 us (12%)
    pallas_call x1, Pallas kernels, bwd_call(): pl.pallas_call(functools.partial(bwd_kernel, dims), out_shape=(S((2, dim)...  156 us
    pallas_call x1, Pallas kernels, fwd_call(): pl.pallas_call(functools.partial(fwd_kernel, dims), out_shape=(S((inner +...  86.7 us
    unnamed x33, local copies, waits for them, and re-layouts  25.1 us

profile of v1, /device:TPU:21, one launch (start us, length us, event | category | flops | bytes accessed | tf_op | source)
XLA Modules:
  0.0 278.3 jit_solution(12284093146739297048)
XLA Ops:
  1.4 0.7 stack.9
  2.1 0.7 stack.10
  2.8 0.6 pad_maximum_fusion.g_ref
  3.4 2.5 copy.27.wq_hbm
  5.8 1.4 copy.28.wk_hbm
  7.3 1.4 copy.29.wv_hbm
  8.7 86.7 %attn_fwd.1 = (f32[392,256]{1,0:T(8,128)}, bf16[128,768]{1,0:T(8,128)(2,1)}, bf16[128,768]{1,0:T(8,128)(2,1)}, f32[128,768]{1,0:T(8,128)}, f32[8,256]{1,0:T(8,12...) custom-call(s32[1]{0:T(128)S(6)} %copy.42.len_ref, ...), custom_call_target="tpu_custom_call" | custom-call | flops 10000000000 | bytes 31457280 | tf_op jit(solution)/shard_map/attn_fwd/pallas_call | solution.py:1032
  95.4 156.4 %attn_bwd.1 = (f32[2,768]{1,0:T(2,128)}, f32[128,768]{1,0:T(8,128)}, f32[1024,768]{1,0:T(8,128)}, f32[2,3,4,2,16,768]{5,4,3,2,1,0:T(8,128)}, f32[2,3,4,2,16,768]...) custom-call(s32[1]{0:T(128)S(6)} %copy.42.len_ref, ...), custom_call_target="tpu_custom_call" | custom-call | flops 10000000000 | bytes 31457280 | tf_op jit(solution)/shard_map/attn_bwd/pallas_call | solution.py:767
  251.8 1.4 slice_reduce_fusion
  253.2 1.8 copy.43
  254.9 3.9 %copy.44 = f32[1024,768]{1,0:T(8,128)} copy(f32[1024,768]{1,0:T(8,128)} %get-tuple-element.69) | data formatting | bytes 6291456
  258.9 1.4 copy.45
  260.3 1.1 copy-done.2
  261.4 1.4 copy.46
  262.8 1.4 copy.47
  264.2 1.8 copy-done
  265.9 1.4 copy.48
  267.4 0.0 slice-start
  267.4 3.2 %copy.49 = f32[768,2048]{1,0:T(8,128)} copy(f32[768,2048]{1,0:T(8,128)S(1)} %bitcast.23) | data formatting | bytes 12582912
  270.6 0.1 slice-done.2
  270.7 1.3 slice-done.3
  272.0 2.9 %copy.50 = f32[768,2048]{1,0:T(8,128)} copy(f32[768,2048]{1,0:T(8,128)S(1)} %bitcast.21) | data formatting | bytes 12582912
  274.9 0.7 slice-done.1
  275.6 2.7 copy.51
  (21 shorter events, 0.0 us)
Async XLA Ops:
  0.6 5.2 %copy-start.4 = (bf16[768,12,64]{0,2,1:T(8,128)(2,1)S(1)}, bf16[768,12,64]{0,2,1:T(8,128)(2,1)}, u32[]{:S(2)}) copy-start(bf16[768,12,64]{0,2,1:T(8,128)(2,1)} %param.19) | copy-start | bytes 3538948
  3.4 3.9 %copy-start.5 = (bf16[768,12,64]{0,2,1:T(8,128)(2,1)S(1)}, bf16[768,12,64]{0,2,1:T(8,128)(2,1)}, u32[]{:S(2)}) copy-start(bf16[768,12,64]{0,2,1:T(8,128)(2,1)} %param.20) | copy-start | bytes 3538948
  254.9 3.9 %copy-start.3 = (f32[768,768]{1,0:T(8,128)S(1)}, f32[768,768]{1,0:T(8,128)}, u32[]{:S(2)}) copy-start(f32[768,768]{1,0:T(8,128)} %get-tuple-element.48) | copy-start | bytes 7077892
  258.8 2.5 copy-start.2
  258.8 3.9 %copy-start.1 = (f32[2,3,4,2,16,768]{5,4,3,2,1,0:T(8,128)S(1)}, f32[2,3,4,2,16,768]{5,4,3,2,1,0:T(8,128)}, u32[]{:S(2)}) copy-start(f32[2,3,4,2,16,768]{5,4,3,2,1,0:T(8,128)} %get-tuple-element.50) | copy-start | bytes 7077892
  261.4 6.0 %slice-start.4 = ((s8[6291456]{0:T(1024)(128)(4,1)}), s8[4194304]{0:T(1024)(128)(4,1)S(1)}, s32[]{:S(2)}) async-start(s8[6291456]{0:T(1024)(128)(4,1)} %bitcast.22), calls=%async_computation.4 | async-start | bytes 8388608
  262.8 3.2 %copy-start = (f32[768,768]{1,0:T(8,128)S(1)}, f32[768,768]{1,0:T(8,128)}, u32[]{:S(2)}) copy-start(f32[768,768]{1,0:T(8,128)} %get-tuple-element.51) | copy-start | bytes 7077892
  262.8 4.6 %slice-start.5 = ((s8[6291456]{0:T(1024)(128)(4,1)}), s8[2097152]{0:T(1024)(128)(4,1)S(1)}, s32[]{:S(2)}) async-start(s8[6291456]{0:T(1024)(128)(4,1)} %bitcast.22), calls=%async_computation.5 | async-start | bytes 4194304
  265.9 4.7 %slice-start.2 = ((s8[6291456]{0:T(1024)(128)(4,1)}), s8[4194304]{0:T(1024)(128)(4,1)S(1)}, s32[]{:S(2)}) async-start(s8[6291456]{0:T(1024)(128)(4,1)} %bitcast.20), calls=%async_computation.2 | async-start | bytes 8388608
  267.3 4.6 %slice-start.3 = ((s8[6291456]{0:T(1024)(128)(4,1)}), s8[2097152]{0:T(1024)(128)(4,1)S(1)}, s32[]{:S(2)}) async-start(s8[6291456]{0:T(1024)(128)(4,1)} %bitcast.20), calls=%async_computation.3 | async-start | bytes 4194304
  267.4 7.5 %slice-start = ((s8[6291456]{0:T(1024)(128)(4,1)}), s8[4194304]{0:T(1024)(128)(4,1)S(1)}, s32[]{:S(2)}) async-start(s8[6291456]{0:T(1024)(128)(4,1)} %bitcast.18), calls=%async_computation | async-start | bytes 8388608
  272.0 3.6 %slice-start.1 = ((s8[6291456]{0:T(1024)(128)(4,1)}), s8[2097152]{0:T(1024)(128)(4,1)S(1)}, s32[]{:S(2)}) async-start(s8[6291456]{0:T(1024)(128)(4,1)} %bitcast.18), calls=%async_computation.1 | async-start | bytes 4194304

commit v2 on v1

--- a/solution.py
+++ b/solution.py
@@ -87,69 +87,69 @@
     ("b", 20): [("dq0", 1, 0, 2), ("att", 0, 1, 2)],
     ("b", 21): [("dq0", 0, 0, 2), ("dq0", 1, 1, 2)],
     ("b", 22): [("att", 0, 0, 3), ("att", 1, 1, 3)],
-    ("b", 23): [("dq0", 0, 1, 1), ("ar0", 0, 1, 3), ("ar0", 1, 0, 3), ("ar0", 0, 0, 4), ("ar0", 1, 1, 4), ("att", 1, 0, 3)],
-    ("b", 24): [("dq0", 1, 0, 1), ("dq1", 0, 0, 4), ("att", 0, 1, 3)],
-    ("b", 25): [("dq0", 0, 0, 1), ("dq0", 1, 1, 1), ("dq1", 1, 1, 4)],
+    ("b", 23): [("dq0", 0, 1, 1), ("att", 1, 0, 3), ("ar0", 0, 1, 3), ("ar0", 1, 0, 3), ("ar0", 0, 0, 4), ("ar0", 1, 1, 4)],
+    ("b", 24): [("dq1", 0, 0, 4), ("dq0", 1, 0, 1), ("att", 0, 1, 3)],
+    ("b", 25): [("dq1", 1, 1, 4), ("dq0", 0, 0, 1), ("dq0", 1, 1, 1)],
     ("b", 26): [("att", 0, 0, 4), ("att", 1, 1, 4)],
-    ("b", 27): [("dq0", 0, 1, 0), ("dq1", 0, 1, 3), ("ar0", 1, 0, 2)],
+    ("b", 27): [("dq1", 0, 1, 3), ("dq0", 0, 1, 0), ("ar0", 1, 0, 2)],
     ("b", 28): [("dq1", 1, 0, 3), ("ar0", 1, 1, 3), ("ar0", 0, 1, 2)],
     ("b", 29): [("dq0", 1, 0, 0), ("ar0", 0, 0, 3)],
-    ("b", 30): [("dq0", 1, 1, 0), ("dq1", 0, 0, 3)],
-    ("b", 31): [("dq0", 0, 0, 0), ("ds0", "start"), ("dq1", 1, 1, 3), ("ar0", 1, 0, 1)],
+    ("b", 30): [("dq1", 0, 0, 3), ("dq1", 1, 1, 3)],
+    ("b", 31): [("dq0", 0, 0, 0), ("dq0", 1, 1, 0), ("ds0", "start"), ("ar0", 1, 0, 1)],
     ("b", 32): [("dq1", 0, 1, 2), ("dq1", 1, 0, 2), ("ar0", 0, 1, 1)],
     ("b", 33): [("ar0", 0, 0, 2), ("ar0", 1, 1, 2)],
-    ("b", 34): [("dq1", 0, 0, 2), ("ds0", 1, 1, 1), ("ds0", 1, 0, 1)],
-    ("b", 35): [("dq1", 1, 1, 2), ("dq1", 0, 1, 1), ("ar0", 1, 0, 0), ("ar1", 0, 1, 3), ("ar1", 1, 0, 3), ("ar1", 0, 0, 4), ("ar1", 1, 1, 4), ("ds0", 0, 0, 1), ("ds0", 0, 1, 1)],
-    ("b", 36): [("dq1", 1, 0, 1), ("dq2", 0, 0, 4), ("ar0", 0, 1, 0), ("ar0", 0, 0, 1), ("ar0", 1, 1, 1)],
-    ("b", 37): [("dq1", 0, 0, 1), ("dq2", 1, 1, 4), ("ds0", 1, 1, 2), ("ds0", 1, 0, 2)],
-    ("b", 38): [("dq1", 0, 1, 0), ("dq1", 1, 1, 1)],
-    ("b", 39): [("dq2", 0, 1, 3), ("ar1", 0, 1, 2), ("ar1", 1, 0, 2)],
-    ("b", 40): [("dq2", 1, 0, 3), ("ar1", 0, 0, 3), ("ar1", 1, 1, 3), ("ds0", 0, 0, 2)],
-    ("b", 41): [("dq1", 1, 0, 0), ("ds0", 0, 1, 2)],
+    ("b", 34): [("dq1", 0, 0, 2), ("dq1", 1, 1, 2)],
+    ("b", 35): [("dq1", 0, 1, 1), ("ds0", 0, 0, 1), ("ds0", 1, 1, 1), ("ds0", 0, 1, 1), ("ds0", 1, 0, 1), ("ar1", 0, 1, 3), ("ar1", 1, 0, 3), ("ar1", 0, 0, 4), ("ar1", 1, 1, 4), ("ar0", 1, 0, 0)],
+    ("b", 36): [("dq2", 0, 0, 4), ("dq1", 1, 0, 1), ("ar0", 0, 1, 0), ("ar0", 0, 0, 1), ("ar0", 1, 1, 1)],
+    ("b", 37): [("dq2", 1, 1, 4), ("dq1", 0, 0, 1), ("dq1", 1, 1, 1)],
+    ("b", 38): [("dq1", 0, 1, 0), ("ds0", 1, 1, 2), ("ds0", 1, 0, 2)],
+    ("b", 39): [("dq2", 0, 1, 3), ("ds0", 0, 0, 2), ("ds0", 0, 1, 2), ("ar1", 1, 0, 2)],
+    ("b", 40): [("dq2", 1, 0, 3), ("ar1", 1, 1, 3), ("ar1", 0, 1, 2)],
+    ("b", 41): [("dq1", 1, 0, 0), ("ar1", 0, 0, 3)],
     ("b", 42): [("dq2", 0, 0, 3), ("ar0", 1, 1, 0)],
-    ("b", 43): [("dq2", 1, 1, 3), ("ar0", 0, 0, 0), ("as0", "start"), ("ds0", 1, 1, 3), ("dq1", 0, 0, 0), ("ds0", 1, 0, 3)],
-    ("b", 45): [("dq1", 1, 1, 0), ("ds1", "start"), ("dq2", 0, 1, 2), ("ar1", 0, 1, 1), ("ar1", 1, 0, 1)],
-    ("b", 46): [("dq2", 1, 0, 2), ("ar1", 0, 0, 2), ("ds0", 0, 0, 3)],
-    ("b", 47): [("dq2", 0, 0, 2), ("dq2", 1, 1, 2), ("ar1", 1, 1, 2), ("ar2", 0, 1, 3), ("ar2", 1, 0, 3), ("ar2", 0, 0, 4), ("ar2", 1, 1, 4), ("ds0", 0, 1, 3)],
+    ("b", 43): [("dq2", 1, 1, 3), ("ar0", 0, 0, 0), ("as0", "start")],
+    ("b", 44): [("dq1", 0, 0, 0), ("dq1", 1, 1, 0), ("ds1", "start"), ("ds0", 1, 1, 3)],
+    ("b", 45): [("dq2", 0, 1, 2), ("ds0", 1, 0, 3), ("ds0", 0, 0, 3), ("ar1", 1, 0, 1), ("ds0", 0, 1, 3)],
+    ("b", 46): [("dq2", 1, 0, 2), ("ar1", 0, 1, 1)],
+    ("b", 47): [("dq2", 0, 0, 2), ("dq2", 1, 1, 2), ("ar2", 0, 1, 3), ("ar2", 1, 0, 3), ("ar2", 0, 0, 4), ("ar2", 1, 1, 4), ("ar1", 0, 0, 2), ("ar1", 1, 1, 2)],
     ("b", 5): [("dh", 0, 0, 2), ("dh", 1, 1, 2)],
     ("b", 6): [("dh", 0, 1, 2), ("dh", 1, 0, 2), ("st", 0, 0, 2), ("st", 1, 1, 2)],
     ("b", 7): [("st", 0, 1, 2), ("st", 1, 0, 2)],
     ("b", 9): [("dh", 0, 0, 3), ("dh", 1, 1, 3)],
-    ("f", 1): [("dq2", 0, 0, 1), ("ar1", 1, 1, 1), ("ar2", 0, 1, 2), ("ar2", 1, 0, 2)],
-    ("f", 10): [("dq2", 1, 1, 0), ("ar1", 0, 0, 0)],
-    ("f", 12): [("dq2", 0, 0, 0), ("ds2", "start"), ("ar1", 1, 1, 0), ("as1", "start")],
-    ("f", 14): [("ar2", 0, 1, 1), ("ar2", 1, 0, 1)],
-    ("f", 16): [("ar2", 0, 0, 2), ("ar2", 1, 1, 2)],
-    ("f", 17): [("as0", 0, 0, 3), ("as0", 1, 1, 3), ("as0", 0, 1, 3), ("as0", 1, 0, 3), ("ds1", 0, 0, 3), ("ds1", 1, 1, 3), ("ds1", 0, 1, 3), ("ds1", 1, 0, 3)],
-    ("f", 19): [("ds2", 0, 0, 1), ("ds2", 1, 1, 1)],
+    ("f", 1): [("ar2", 0, 1, 2), ("ar2", 1, 0, 2), ("ar2", 0, 0, 3), ("ar2", 1, 1, 3)],
+    ("f", 10): [("dq2", 0, 0, 0), ("dq2", 1, 1, 0), ("ds2", "start")],
+    ("f", 12): [("ar2", 0, 1, 1), ("ar2", 1, 0, 1)],
+    ("f", 14): [("ar2", 0, 0, 2), ("ar2", 1, 1, 2)],
+    ("f", 17): [("ds1", 0, 0, 3), ("ds1", 1, 1, 3), ("ar1", 0, 0, 0), ("ar1", 1, 1, 0), ("as1", "start"), ("as0", 0, 0, 3), ("as0", 1, 1, 3), ("as0", 0, 1, 3), ("as0", 1, 0, 3)],
+    ("f", 19): [("ds1", 0, 1, 3), ("ds1", 1, 0, 3), ("ds2", 0, 0, 1), ("ds2", 1, 1, 1)],
     ("f", 21): [("ds2", 0, 1, 1), ("ds2", 1, 0, 1)],
-    ("f", 23): [("as1", 0, 0, 1), ("as1", 1, 1, 1)],
-    ("f", 25): [("as1", 0, 1, 1), ("as1", 1, 0, 1)],
-    ("f", 26): [("ar2", 0, 1, 0), ("ar2", 1, 0, 0), ("ar2", 0, 0, 1), ("ar2", 1, 1, 1), ("as0", 0, 0, 4), ("as0", 1, 1, 4), ("ds1", 0, 0, 4), ("ds1", 1, 1, 4)],
-    ("f", 28): [("ds2", 0, 0, 2), ("ds2", 1, 1, 2)],
-    ("f", 3): [("ar2", 0, 0, 3), ("ar2", 1, 1, 3)],
-    ("f", 30): [("ds2", 0, 1, 2), ("ds2", 1, 0, 2)],
-    ("f", 32): [("as1", 0, 0, 2), ("as1", 1, 1, 2)],
-    ("f", 34): [("as1", 0, 1, 2), ("as1", 1, 0, 2)],
-    ("f", 35): [("ar2", 0, 0, 0), ("ar2", 1, 1, 0), ("as2", "start"), ("ds2", 0, 0, 3), ("as1", 0, 0, 3), ("ds2", 1, 1, 3), ("as1", 1, 1, 3), ("ds2", 0, 1, 3), ("ds2", 1, 0, 3)],
+    ("f", 23): [("ar2", 0, 1, 0), ("ar2", 1, 0, 0)],
+    ("f", 25): [("ar2", 0, 0, 1), ("ar2", 1, 1, 1)],
+    ("f", 26): [("ds1", 0, 0, 4), ("ds1", 1, 1, 4), ("as1", 0, 0, 1), ("as1", 1, 1, 1), ("as1", 0, 1, 1), ("as1", 1, 0, 1)],
+    ("f", 28): [("as0", 0, 0, 4), ("as0", 1, 1, 4)],
+    ("f", 3): [("ar1", 0, 0, 1), ("ar1", 1, 1, 1)],
+    ("f", 30): [("ds2", 0, 0, 2), ("ds2", 1, 1, 2)],
+    ("f", 32): [("ds2", 0, 1, 2), ("ds2", 1, 0, 2)],
+    ("f", 34): [("ar2", 0, 0, 0), ("ar2", 1, 1, 0), ("as2", "start")],
+    ("f", 35): [("ds2", 0, 0, 3), ("ds2", 1, 1, 3), ("ds2", 0, 1, 3), ("ds2", 1, 0, 3), ("as1", 0, 0, 2), ("as1", 1, 1, 2), ("as1", 0, 1, 2), ("as1", 1, 0, 2)],
     ("f", 5): [("as0", 0, 0, 2), ("as0", 1, 1, 2)],
     ("f", 7): [("as0", 0, 1, 2), ("as0", 1, 0, 2)],
     ("f", 8): [("dq2", 0, 1, 0), ("dq2", 1, 0, 0), ("ds1", 0, 0, 2), ("ds1", 1, 1, 2), ("ds1", 0, 1, 2), ("ds1", 1, 0, 2)],
     ("h", 0): [("as0", 0, 0, 1), ("as0", 1, 1, 1)],
-    ("h", 1): [("as0", 0, 1, 1), ("as0", 1, 0, 1), ("ds1", 0, 0, 1), ("ds0", 1, 1, 4)],
-    ("h", 2): [("ds1", 0, 1, 1), ("ds1", 1, 1, 1)],
-    ("h", 3): [("ds1", 1, 0, 1)],
-    ("h", 4): [("dq2", 0, 1, 1), ("ar1", 1, 0, 0)],
-    ("h", 5): [("ar1", 0, 1, 0), ("dq2", 1, 0, 1)],
-    ("h", 6): [("ar1", 0, 0, 1), ("ds0", 0, 0, 4)],
-    ("h", 7): [("dq2", 1, 1, 1)],
-    ("m", 1): [("as1", 0, 1, 3), ("as1", 1, 0, 3)],
-    ("m", 3): [("as2", 0, 0, 1), ("as2", 1, 1, 1)],
-    ("m", 4): [("ds2", 0, 0, 4), ("ds2", 1, 1, 4)],
-    ("q", 0): [("as2", 0, 1, 1), ("as2", 1, 0, 1)],
-    ("q", 1): [("as1", 0, 0, 4), ("as1", 1, 1, 4)],
+    ("h", 1): [("as0", 0, 1, 1), ("as0", 1, 0, 1)],
+    ("h", 2): [("ds1", 0, 0, 1), ("ds1", 1, 1, 1), ("ds1", 0, 1, 1), ("ds1", 1, 0, 1)],
+    ("h", 3): [("ds0", 1, 1, 4)],
+    ("h", 4): [("dq2", 0, 1, 1), ("ar1", 1, 0, 0), ("ds0", 0, 0, 4)],
+    ("h", 6): [("dq2", 1, 0, 1), ("ar1", 0, 1, 0)],
+    ("h", 7): [("dq2", 0, 0, 1), ("dq2", 1, 1, 1)],
+    ("m", 0): [("as2", 0, 0, 1), ("as2", 1, 1, 1)],
+    ("m", 1): [("as2", 0, 1, 1), ("as2", 1, 0, 1)],
+    ("m", 3): [("ds2", 0, 0, 4), ("ds2", 1, 1, 4)],
+    ("q", 0): [("as1", 0, 0, 3), ("as1", 1, 1, 3)],
+    ("q", 2): [("as1", 0, 1, 3), ("as1", 1, 0, 3)],
     ("q", 3): [("as2", 0, 0, 2), ("as2", 1, 1, 2)],
-    ("q", 6): [("as2", 0, 1, 2), ("as2", 1, 0, 2)],
+    ("q", 5): [("as2", 0, 1, 2), ("as2", 1, 0, 2)],
+    ("q", 7): [("as1", 0, 0, 4), ("as1", 1, 1, 4)],
     ("q", 8): [("as2", 0, 0, 3), ("as2", 1, 1, 3), ("as2", 0, 1, 3), ("as2", 1, 0, 3), ("as2", 0, 0, 4), ("as2", 1, 1, 4)],
     ("r", 12): [("dh", 0, 0, 4), ("dh", 1, 1, 4), ("att", "start"), ("st", 0, 0, 4), ("st", 1, 1, 4)],
 }
@@ -331,12 +331,12 @@
     return hi, mid, lo
 
 
-def bwd_kernel(dims, len_ref, dh_ref, own_ref, gn_ref, att_ref, y_ref, gh_ref, g_ref,
+def bwd_kernel(dims, len_ref, dh_ref, own_ref, gn_ref, att_ref, y_ref, gh_ref, g1_ref, g2_ref,
                k_hbm, v_hbm, kt_hbm, qz_hbm, wo_hbm, wq_hbm, wk_hbm, wv_hbm, ma_hbm, mb_hbm, y_hbm, gog, wg_hbm, wu_hbm, wd_hbm,
                gvec_ref, gdec_ref, gmem, gwk, gwv, gwq, gwo, gdown, ggate, gup, attg,
                dqo_ref, k_ref, v_ref, kt_ref, qz_ref, wo_ref, wq_ref, wk_ref, wv_ref, ak_ref,
                dhg, doz, aqs, ads, stb, dk, dv, dkv, dkvp, dqp, dqr, dqa, arp, arr, ara, pvec, pdq, spb,
-               msc, ybuf, abuf, wbuf, dbuf, wt, gst, gsw, gwo_s, gwq_s,
+               msc, ybuf, abuf, wbuf, dbuf, wt, gst, gsw, gwo_s,
                *sems):
     chips, rows, mem, dim, hc, c, ff = dims
     QT = 2 * rows
@@ -530,7 +530,7 @@
         cp.wait()
     for off in near:
         att_g.ready(off)
-    gain2 = g_ref[1:2, :].astype(F32)
+    gain2 = g2_ref[...].astype(F32)[None, :]
     gwo_s[...] = jnp.zeros_like(gwo_s)
 
     def y_fetch(ch, slot):
@@ -678,9 +678,11 @@
     lax.fori_loop(0, nb, memory_rows, 0)
     run("m", nb)
 
-    gain = g_ref[0:1, :].astype(F32)
+    gain = g1_ref[...].astype(F32)[None, :]
     y_fetch(0, 0).start()
     spb[...] = jnp.zeros_like(spb)
+    both_wait(wo_out)
+    gwq_s = gwo_s
     gwq_s[...] = jnp.zeros_like(gwq_s)
     wq_h = wq_ref[:, hcol]
 
@@ -736,7 +738,6 @@
         xp(p).wait_send()
     cv.wait()
     gvec_ref[...] = spb[0:2] + pvec[0:2]
-    both_wait(wo_out)
     both_wait(wq_out)
     for cp in wkv_out:
         cp.wait()
@@ -768,7 +769,7 @@
         functools.partial(bwd_kernel, dims),
         out_shape=(S((2, dim), F32), S((rows, dim), F32), S((mem, dim), F32), S((2, np_, chips // 2, 2, seg, dim), F32), S((2, np_, chips // 2, 2, seg, dim), F32), S((2 * inner, dim), F32), S((2 * inner, dim), F32),
                    S((ff, dim), F32), S((dim, ff), F32), S((dim, ff), F32), S(gshape, BF16)),
-        in_specs=[pl.BlockSpec(memory_space=pltpu.SMEM)] + [v] * 7 + [hbm] * 15, out_specs=(v,) * 2 + (hbm,) * 9,
+        in_specs=[pl.BlockSpec(memory_space=pltpu.SMEM)] + [v] * 8 + [hbm] * 15, out_specs=(v,) * 2 + (hbm,) * 9,
         scratch_shapes=[
             VMEM((2 * inner, rows), BF16), VMEM((T, inner), BF16), VMEM((T, inner), BF16), VMEM((inner, T), BF16), VMEM((hc * 128, cols), BF16), VMEM((2 * inner, dim), BF16), wsq, wsq, wsq, VMEM((T, 128), BF16),
             VMEM(gshape, BF16), VMEM((max(hc * 128, 3 * FT), cols), BF16), VMEM((hc * 16, cols), BF16), VMEM((hc * 16, cols), BF16),
@@ -778,14 +779,53 @@
             VMEM((8, dim), F32), VMEM((np_, 2, 64, rows), BF16), VMEM((8, dim), F32),
             VMEM((2, mem, dim), BF16), VMEM((2, 2, 2, rows // 2, dim), BF16), VMEM((2, 2, 2, rows // 2, dim), BF16),
             VMEM((2, dim, FT), BF16), VMEM((2, FT, dim), BF16), VMEM((2, FT, dim), BF16), VMEM((2, max(FT, mem // 4), dim), F32), VMEM((2, 2, dim, FT), F32),
-            VMEM((inner, dim), F32), VMEM((inner, dim), F32)]
+            VMEM((inner, dim), F32)]
         + rows_sems * 2 + two * (1 + 4 * np_) + [DMA((4 * np_ + 1,))] * 2 + [DMA((2 + 2 * np_,)), DMA((14,)), DMA((14,)), DMA((16,)), DMA((2, 3)), DMA((2, 2)), DMA((10,))],
         compiler_params=pltpu.CompilerParams(vmem_limit_bytes=67_043_328, collective_id=1, has_side_effects=True),
         cost_estimate=pl.CostEstimate(flops=10**10, bytes_accessed=30 << 20, transcendentals=0),
         name="attn_bwd")(*args)
 
 
-def fwd_kernel(dims, len_ref, y_ref, go_ref, m_ref, g_ref, wq_hbm, wk_hbm, wv_hbm, wo_hbm, wg_hbm, wu_hbm, wd_hbm,
+def finish_kernel(slots, *refs):
+    n = (len(refs) - 3) // 2
+    srcs, dsts, (buf, si, so) = refs[:n], refs[n:2 * n], refs[2 * n:]
+    rows = buf.shape[1]
+    moves = []
+    for src, dst in zip(srcs, dsts):
+        for c in range(0, src.shape[1], buf.shape[2]):
+            wide = min(buf.shape[2], src.shape[1] - c)
+            cols = pl.ds(c, wide)
+            for r in range(0, src.shape[0], rows):
+                k = len(moves) % slots
+                w = min(rows, src.shape[0] - r)
+                b = buf.at[k, pl.ds(0, w), pl.ds(0, wide)]
+                moves.append((pltpu.make_async_copy(src.at[pl.ds(r, w), cols], b, si.at[k]), pltpu.make_async_copy(b, dst.at[pl.ds(r, w), cols], so.at[k])))
+    lag = slots // 2
+    for i in range(len(moves) + lag):
+        if i < len(moves):
+            if i >= slots:
+                moves[i - slots][1].wait()
+            moves[i][0].start()
+        if i >= lag:
+            moves[i - lag][0].wait()
+            moves[i - lag][1].start()
+    for m in moves[-slots:]:
+        m[1].wait()
+
+
+def finish_call(*arrays):
+    slots, rows, cols = 16, 256, 1024
+    hbm = pl.BlockSpec(memory_space=pl.ANY)
+    return pl.pallas_call(
+        functools.partial(finish_kernel, slots),
+        out_shape=tuple(jax.ShapeDtypeStruct(a.shape, a.dtype) for a in arrays),
+        in_specs=[hbm] * len(arrays), out_specs=(hbm,) * len(arrays),
+        scratch_shapes=[VMEM((slots, rows, cols), F32), DMA((slots,)), DMA((slots,))],
+        compiler_params=pltpu.CompilerParams(vmem_limit_bytes=32 * 1024 * 1024),
+        name="finish")(*arrays)
+
+
+def fwd_kernel(dims, len_ref, y_ref, go_ref, m_ref, g1_ref, g2_ref, wq_hbm, wk_hbm, wv_hbm, wo_hbm, wg_hbm, wu_hbm, wd_hbm,
                own, att_ref, dh_ref, gh_ref, gn_ref, k_out, v_out, kt_out, qz_out, mg_out, yall, gog,
                k_s, v_s, kt_s, qz, mg, wq_ref, wk_ref, wv_ref, ak_ref, yg, wqt, vt_s, s_scr, mx_scr, part, rbuf, patt, satt, gob, attt, wo_s, wg_s, wu_s, wd_s, n2_s, dn_s, *sems):
     chips, rows, mem, dim, hc, c, ff = dims
@@ -871,7 +911,7 @@
     run("s", 2)
     for cp in stores[:4]:
         cp.start()
-    gain = g_ref[0:1, :].astype(F32)
+    gain = g1_ref[...].astype(F32)[None, :]
     one_row = jnp.where(lax.broadcasted_iota(jnp.int32, (16, QT), 0) == 0, 1.0, 0.0).astype(BF16)
 
     def lanes(chip):
@@ -973,7 +1013,7 @@
 
     att = attt[...].T
     att_ref[...] = att
-    gain2 = g_ref[1:2, :].astype(F32)
+    gain2 = g2_ref[...].astype(F32)[None, :]
     run("t", 3)
     hid = (y_ref[...].astype(F32) + mm(att, wo_s[...])).astype(BF16).astype(F32)
     inv = lax.rsqrt(jnp.mean(hid * hid, axis=-1, keepdims=True) + 1e-6)
@@ -1033,7 +1073,7 @@
         functools.partial(fwd_kernel, dims),
         out_shape=(S((inner + 8, QT), F32), S((rows, 2 * inner), BF16), S((rows, dim), BF16), S((rows, dim), F32), S((8, QT), F32),
                    S((T, inner), BF16), S((T, inner), BF16), S((inner, T), BF16), S((hc * 128, chips * QT), BF16), S((mem, dim), BF16), S(gshape, BF16), S(gshape, BF16)),
-        in_specs=[pl.BlockSpec(memory_space=pltpu.SMEM)] + [v] * 4 + [hbm] * 7, out_specs=(v,) * 5 + (hbm,) * 7,
+        in_specs=[pl.BlockSpec(memory_space=pltpu.SMEM)] + [v] * 5 + [hbm] * 7, out_specs=(v,) * 5 + (hbm,) * 7,
         scratch_shapes=[
             VMEM((T, inner), BF16), VMEM((T, inner), BF16), VMEM((inner, T), BF16), VMEM((hc * 128, chips * QT), BF16), VMEM((mem, dim), BF16),
             VMEM((dim, 2 * inner), BF16), VMEM((dim, 2 * inner), BF16), VMEM((dim, 2 * inner), BF16), VMEM((T, 128), BF16),
@@ -1064,15 +1104,16 @@
         dims = (chips, rows, mem, dim, hc, c, w_gate.shape[1])
         wq2, wk2, wv2 = (w.reshape(dim, inner) for w in (wq, wk, wv))
         wo2 = wo.reshape(inner, dim)
-        gains = jnp.stack([norm_attn, norm_mlp])
 
         own, attended, dh, grad_hidden, gn, k_c, v_c, kt_c, qz, mem_p, y_all, go_all = fwd_call(
-            dims, mem_len, dec_in, grad_out, memory, gains, wq2, wk2, wv2, wo2, w_gate, w_up, w_down)
+            dims, mem_len, dec_in, grad_out, memory, norm_attn, norm_mlp, wq2, wk2, wv2, wo2, w_gate, w_up, w_down)
         gvec, g_dec, g_mem, g_wk, g_wv, g_wq, g_wo, g_down, g_gate, g_up, _ = bwd_call(
-            dims, mem_len, dh, own, gn, attended, dec_in, grad_hidden, gains,
+            dims, mem_len, dh, own, gn, attended, dec_in, grad_hidden, norm_attn, norm_mlp,
             k_c, v_c, kt_c, qz, wo2, wq2, wk2, wv2, memory, mem_p, y_all, go_all, w_gate, w_up, w_down)
         cube = (dim, heads, hd)
-        g_wq, g_wk, g_wv = (g.reshape(inner, dim).T.reshape(cube) for g in (g_wq, g_wk, g_wv))
+        g_wk, g_wv = (g.reshape(inner, dim) for g in (g_wk, g_wv))
+        g_mem, g_wq, g_wk, g_wv, g_wo, g_down, g_gate, g_up = finish_call(g_mem, g_wq, g_wk, g_wv, g_wo, g_down, g_gate, g_up)
+        g_wq, g_wk, g_wv = (g.T.reshape(cube) for g in (g_wq, g_wk, g_wv))
         return (g_dec, g_mem, gvec[0], g_wq, g_wk, g_wv, g_wo.reshape(heads, hd, dim), gvec[1], g_gate, g_up, g_down)
 
     return jax.shard_map(device_step, mesh=mesh,

time: 279 us -> 279 us (level)
  Pallas kernels: 243 us -> 259 us
  local copies, waits for them, and re-layouts: 33.2 us -> 18.1 us
    pallas_call x0 -> x1, Pallas kernels: none -> 16.1 us  [finish_call(): pl.pallas_call(functools.partial(finish_kernel, slots), out_shape=tuple((...]
    unnamed x33 -> x21, local copies, waits for them, and re-layouts: 25.1 us -> 12.1 us
where the time goes in v2:
time: 279 us; the launch traced here: 278 us
  Pallas kernels  259 us (93%)
  local copies, waits for them, and re-layouts  18.1 us (6%)
    pallas_call x1, Pallas kernels, bwd_call(): pl.pallas_call(functools.partial(bwd_kernel, dims), out_shape=(S((2, dim)...  156 us
    pallas_call x1, Pallas kernels, fwd_call(): pl.pallas_call(functools.partial(fwd_kernel, dims), out_shape=(S((inner +...  86.7 us
    pallas_call x1, Pallas kernels, finish_call(): pl.pallas_call(functools.partial(finish_kernel, slots), out_shape=tuple((...  16.1 us
    unnamed x21, local copies, waits for them, and re-layouts  12.1 us

profile of v2, /device:TPU:21, one launch (start us, length us, event | category | flops | bytes accessed | tf_op | source)
XLA Modules:
  0.0 278.4 jit_solution(12828972011236997276)
XLA Ops:
  0.6 0.0 copy-start.6
  0.7 0.0 copy-start.7
  0.7 2.5 copy.27.wq_hbm
  3.2 0.0 copy-done.6
  3.2 1.4 copy.28.wk_hbm
  4.6 0.0 copy-done.7
  4.6 1.4 copy.29.wv_hbm
  6.7 86.7 %attn_fwd.1 = (f32[392,256]{1,0:T(8,128)}, bf16[128,768]{1,0:T(8,128)(2,1)}, bf16[128,768]{1,0:T(8,128)(2,1)}, f32[128,768]{1,0:T(8,128)}, f32[8,256]{1,0:T(8,12...) custom-call(s32[1]{0:T(128)S(6)} %copy.34.len_ref, ...), custom_call_target="tpu_custom_call" | custom-call | flops 10000000000 | bytes 31457280 | tf_op jit(solution)/shard_map/attn_fwd/pallas_call | solution.py:1072
  93.5 156.0 %attn_bwd.1 = (f32[2,768]{1,0:T(2,128)}, f32[128,768]{1,0:T(8,128)}, f32[1024,768]{1,0:T(8,128)}, f32[2,3,4,2,16,768]{5,4,3,2,1,0:T(8,128)}, f32[2,3,4,2,16,768]...) custom-call(s32[1]{0:T(128)S(6)} %copy.34.len_ref, ...), custom_call_target="tpu_custom_call" | custom-call | flops 10000000000 | bytes 31457280 | tf_op jit(solution)/shard_map/attn_bwd/pallas_call | solution.py:768
  249.5 0.0 copy-start
  249.5 2.8 copy-done
  252.3 0.0 copy-start.1
  252.3 1.9 copy-done.1
  254.2 0.0 copy-start.2
  254.2 1.7 copy-done.2
  255.9 1.7 copy-done.3
  257.5 0.0 copy-start.4
  257.5 1.7 copy-done.4
  259.2 1.7 copy-done.5
  260.9 16.1 %finish.1 = (f32[1024,768]{1,0:T(8,128)}, f32[768,768]{1,0:T(8,128)}, f32[768,768]{1,0:T(8,128)}, f32[768,768]{1,0:T(8,128)}, f32[768,768]{1,0:T(8,128)}, /*inde...) custom-call(f32[1024,768]{1,0:T(8,128)S(1)} %copy-done.1, f32[768,768]{1,0:T(8,128)S(1)} %copy-done.4, ...), custom_call_target="tpu_custom_call" | custom-call | tf_op jit(solution)/shard_map/finish/pallas_call | solution.py:819
  277.0 0.0 copy-done.9
  277.0 0.6 slice_reduce_fusion
  277.6 0.0 copy-done.8
  277.6 0.7 copy.35
  (4 shorter events, 0.0 us)
Async XLA Ops:
  0.6 2.5 copy-start.6
  0.7 4.0 %copy-start.7 = (bf16[768,12,64]{0,2,1:T(8,128)(2,1)S(1)}, bf16[768,12,64]{0,2,1:T(8,128)(2,1)}, u32[]{:S(2)}) copy-start(bf16[768,12,64]{0,2,1:T(8,128)(2,1)} %param.20) | copy-start | bytes 3538948
  249.5 2.8 %copy-start = (f32[2048,768]{1,0:T(8,128)S(1)}, f32[2048,768]{1,0:T(8,128)}, u32[]{:S(2)}) copy-start(f32[2048,768]{1,0:T(8,128)} %get-tuple-element.59.refs_5_) | copy-start | bytes 18874372
  252.3 1.9 copy-start.1
  254.2 1.7 copy-start.2
  255.9 1.7 copy-start.3
  257.5 1.7 copy-start.4
  259.2 1.7 copy-start.5
  260.9 16.2 %copy-start.9 = (f32[2,768]{1,0:T(2,128)S(1)}, f32[2,768]{1,0:T(2,128)}, u32[]{:S(2)}) copy-start(f32[2,768]{1,0:T(2,128)} %get-tuple-element.63) | copy-start | bytes 18436
  260.9 16.8 %copy-start.8 = (f32[128,768]{1,0:T(8,128)S(1)}, f32[128,768]{1,0:T(8,128)}, u32[]{:S(2)}) copy-start(f32[128,768]{1,0:T(8,128)} %get-tuple-element.84) | copy-start | bytes 1179652

commit v3 on v2

--- a/solution.py
+++ b/solution.py
@@ -814,14 +814,14 @@
 
 
 def finish_call(*arrays):
-    slots, rows, cols = 16, 256, 1024
+    slots, rows, cols = 24, 256, 1024
     hbm = pl.BlockSpec(memory_space=pl.ANY)
     return pl.pallas_call(
         functools.partial(finish_kernel, slots),
         out_shape=tuple(jax.ShapeDtypeStruct(a.shape, a.dtype) for a in arrays),
         in_specs=[hbm] * len(arrays), out_specs=(hbm,) * len(arrays),
         scratch_shapes=[VMEM((slots, rows, cols), F32), DMA((slots,)), DMA((slots,))],
-        compiler_params=pltpu.CompilerParams(vmem_limit_bytes=32 * 1024 * 1024),
+        compiler_params=pltpu.CompilerParams(vmem_limit_bytes=67_043_328),
         name="finish")(*arrays)
 
 

time: 279 us -> 275 us (0.986)
  local copies, waits for them, and re-layouts: 18.1 us -> 8.57 us
  Pallas kernels: 259 us -> 264 us
    unnamed x21 -> x5, local copies, waits for them, and re-layouts: 12.1 us -> 1.77 us
    pallas_call x1, Pallas kernels: 16.1 us -> 21.1 us  [finish_call(): pl.pallas_call(functools.partial(finish_kernel, slots), out_shape=tuple((...]
where the time goes in v3:
time: 275 us; the launch traced here: 274 us
  Pallas kernels  264 us (96%)
  local copies, waits for them, and re-layouts  8.57 us (3%)
    pallas_call x1, Pallas kernels, bwd_call(): pl.pallas_call(functools.partial(bwd_kernel, dims), out_shape=(S((2, dim)...  156 us
    pallas_call x1, Pallas kernels, fwd_call(): pl.pallas_call(functools.partial(fwd_kernel, dims), out_shape=(S((inner +...  86.7 us
    pallas_call x1, Pallas kernels, finish_call(): pl.pallas_call(functools.partial(finish_kernel, slots), out_shape=tuple((...  21.1 us

profile of v3, /device:TPU:21, one launch (start us, length us, event | category | flops | bytes accessed | tf_op | source)
XLA Modules:
  0.0 273.8 jit_solution(7130449106830716587)
XLA Ops:
  0.6 0.0 copy-start
  0.7 0.0 copy-start.1
  0.7 2.5 copy.27.wq_hbm
  3.2 0.0 copy-done
  3.2 1.4 copy.28.wk_hbm
  4.6 0.0 copy-done.1
  4.6 1.4 copy.29.wv_hbm
  6.7 86.7 %attn_fwd.1 = (f32[392,256]{1,0:T(8,128)}, bf16[128,768]{1,0:T(8,128)(2,1)}, bf16[128,768]{1,0:T(8,128)(2,1)}, f32[128,768]{1,0:T(8,128)}, f32[8,256]{1,0:T(8,12...) custom-call(s32[1]{0:T(128)S(6)} %copy.34.len_ref, ...), custom_call_target="tpu_custom_call" | custom-call | flops 10000000000 | bytes 31457280 | tf_op jit(solution)/shard_map/attn_fwd/pallas_call | solution.py:1072
  93.5 156.1 %attn_bwd.1 = (f32[2,768]{1,0:T(2,128)}, f32[128,768]{1,0:T(8,128)}, f32[1024,768]{1,0:T(8,128)}, f32[2,3,4,2,16,768]{5,4,3,2,1,0:T(8,128)}, f32[2,3,4,2,16,768]...) custom-call(s32[1]{0:T(128)S(6)} %copy.34.len_ref, ...), custom_call_target="tpu_custom_call" | custom-call | flops 10000000000 | bytes 31457280 | tf_op jit(solution)/shard_map/attn_bwd/pallas_call | solution.py:768
  249.6 21.1 %finish.1 = (f32[1024,768]{1,0:T(8,128)}, f32[768,768]{1,0:T(8,128)}, f32[768,768]{1,0:T(8,128)}, f32[768,768]{1,0:T(8,128)}, f32[768,768]{1,0:T(8,128)}, /*inde...) custom-call(f32[1024,768]{1,0:T(8,128)} %get-tuple-element.54.refs_0_, ...), custom_call_target="tpu_custom_call" | custom-call | tf_op jit(solution)/shard_map/finish/pallas_call | solution.py:819
  270.7 1.4 slice_reduce_fusion
  272.0 1.8 copy.35
Async XLA Ops:
  0.6 2.5 copy-start
  0.7 4.0 %copy-start.1 = (bf16[768,12,64]{0,2,1:T(8,128)(2,1)S(1)}, bf16[768,12,64]{0,2,1:T(8,128)(2,1)}, u32[]{:S(2)}) copy-start(bf16[768,12,64]{0,2,1:T(8,128)(2,1)} %param.20) | copy-start | bytes 3538948

commit v4 on v3

--- a/solution.py
+++ b/solution.py
@@ -36,15 +36,14 @@
 DMA = pltpu.SemaphoreType.DMA
 
 FWD_ORDER = [(0, 0), (0, 1), (1, 0), (1, 1), (-3, 0), (3, 1), (4, 0), (4, 1), (3, 0), (-3, 1), (2, 0), (-2, 1), (2, 1), (-2, 0), (-1, 1), (-1, 0)]
-BWD_ORDER = [0, 1, 4, 3, -3, 2, -2, -1]
+BWD_ORDER = [0, 1, -1, 4, 3, -3, 2, -2]
 BWD_FIRST = 2
 FWD_PLAN = {
     ("b", 0): [("y", 0, 1, 1), ("y", 1, 0, 1)],
     ("b", 11): [("y", 1, 1, 3), ("y", 1, 0, 3)],
-    ("b", 12): [("go", 0, 0, 1)],
-    ("b", 13): [("go", 1, 1, 1)],
+    ("b", 13): [("go", 0, 0, 1), ("go", 1, 1, 1)],
     ("b", 14): [("o", 1, 0, 3)],
-    ("b", 15): [("go", 0, 1, 1)],
+    ("b", 16): [("go", 0, 1, 1)],
     ("b", 17): [("o", 0, 1, 3)],
     ("b", 18): [("go", 1, 0, 1)],
     ("b", 20): [("o", 0, 0, 4)],
@@ -58,10 +57,10 @@
     ("b", 37): [("o", 1, 1, 3)],
     ("b", 38): [("o", 0, 1, 2)],
     ("b", 4): [("y", 0, 0, 2), ("y", 1, 1, 2)],
-    ("b", 40): [("go", 1, 0, 3)],
     ("b", 41): [("o", 1, 0, 2)],
-    ("b", 42): [("go", 0, 1, 3)],
-    ("b", 43): [("go", 1, 1, 4)],
+    ("b", 42): [("go", 1, 0, 3)],
+    ("b", 44): [("go", 0, 1, 3)],
+    ("b", 45): [("go", 1, 1, 4)],
     ("b", 8): [("y", 0, 1, 2), ("y", 1, 0, 2)],
     ("b", 9): [("go", "start")],
     ("r", 3): [("y", 0, 0, 3), ("y", 0, 1, 3)],
@@ -69,89 +68,92 @@
     ("s", 1): [("y", 0, 0, 1), ("y", 1, 1, 1)],
     ("t", 1): [("o", 0, 0, 2), ("o", 1, 1, 2), ("o", 0, 1, 1), ("o", 1, 0, 1), ("o", 0, 0, 1), ("o", 1, 1, 1), ("o", 0, 1, 0), ("o", 1, 0, 0), ("o", 0, 0, 0), ("o", 1, 1, 0)],
     ("t", 2): [("go", 0, 0, 3)],
-    ("t", 6): [("go", 0, 0, 4)],
+    ("t", 7): [("go", 0, 0, 4)],
 }
 BWD_PLAN = {
     ("b", 1): [("dh", 0, 0, 1), ("dh", 1, 1, 1)],
     ("b", 10): [("dh", 0, 1, 3), ("dh", 1, 0, 3), ("st", 0, 0, 3), ("st", 1, 1, 3)],
     ("b", 11): [("st", 0, 1, 3), ("st", 1, 0, 3)],
-    ("b", 12): [("dq0", 0, 0, 4)],
-    ("b", 13): [("dq0", 1, 1, 4)],
-    ("b", 14): [("att", 0, 0, 1), ("att", 1, 1, 1)],
-    ("b", 15): [("dq0", 0, 1, 3), ("att", 0, 1, 1), ("att", 1, 0, 1)],
-    ("b", 16): [("dq0", 0, 0, 3), ("dq0", 1, 0, 3)],
-    ("b", 17): [("dq0", 1, 1, 3)],
-    ("b", 18): [("att", 0, 0, 2), ("att", 1, 1, 2)],
-    ("b", 19): [("dq0", 0, 1, 2), ("att", 1, 0, 2)],
+    ("b", 13): [("dh", 0, 0, 4), ("dh", 1, 1, 4), ("att", "start"), ("st", 0, 0, 4), ("st", 1, 1, 4)],
+    ("b", 14): [("dq0", 0, 0, 4)],
+    ("b", 15): [("dq0", 1, 1, 4)],
+    ("b", 16): [("att", 0, 0, 1), ("att", 1, 1, 1)],
+    ("b", 17): [("dq0", 0, 1, 3)],
+    ("b", 18): [("dq0", 0, 0, 3), ("dq0", 1, 0, 3), ("att", 1, 0, 1), ("att", 0, 1, 1)],
+    ("b", 19): [("dq0", 1, 1, 3)],
     ("b", 2): [("dh", 0, 1, 1), ("dh", 1, 0, 1), ("st", 0, 0, 1), ("st", 1, 1, 1), ("st", 0, 1, 1), ("st", 1, 0, 1)],
-    ("b", 20): [("dq0", 1, 0, 2), ("att", 0, 1, 2)],
-    ("b", 21): [("dq0", 0, 0, 2), ("dq0", 1, 1, 2)],
-    ("b", 22): [("att", 0, 0, 3), ("att", 1, 1, 3)],
-    ("b", 23): [("dq0", 0, 1, 1), ("att", 1, 0, 3), ("ar0", 0, 1, 3), ("ar0", 1, 0, 3), ("ar0", 0, 0, 4), ("ar0", 1, 1, 4)],
-    ("b", 24): [("dq1", 0, 0, 4), ("dq0", 1, 0, 1), ("att", 0, 1, 3)],
-    ("b", 25): [("dq1", 1, 1, 4), ("dq0", 0, 0, 1), ("dq0", 1, 1, 1)],
-    ("b", 26): [("att", 0, 0, 4), ("att", 1, 1, 4)],
-    ("b", 27): [("dq1", 0, 1, 3), ("dq0", 0, 1, 0), ("ar0", 1, 0, 2)],
-    ("b", 28): [("dq1", 1, 0, 3), ("ar0", 1, 1, 3), ("ar0", 0, 1, 2)],
-    ("b", 29): [("dq0", 1, 0, 0), ("ar0", 0, 0, 3)],
-    ("b", 30): [("dq1", 0, 0, 3), ("dq1", 1, 1, 3)],
-    ("b", 31): [("dq0", 0, 0, 0), ("dq0", 1, 1, 0), ("ds0", "start"), ("ar0", 1, 0, 1)],
-    ("b", 32): [("dq1", 0, 1, 2), ("dq1", 1, 0, 2), ("ar0", 0, 1, 1)],
-    ("b", 33): [("ar0", 0, 0, 2), ("ar0", 1, 1, 2)],
-    ("b", 34): [("dq1", 0, 0, 2), ("dq1", 1, 1, 2)],
-    ("b", 35): [("dq1", 0, 1, 1), ("ds0", 0, 0, 1), ("ds0", 1, 1, 1), ("ds0", 0, 1, 1), ("ds0", 1, 0, 1), ("ar1", 0, 1, 3), ("ar1", 1, 0, 3), ("ar1", 0, 0, 4), ("ar1", 1, 1, 4), ("ar0", 1, 0, 0)],
-    ("b", 36): [("dq2", 0, 0, 4), ("dq1", 1, 0, 1), ("ar0", 0, 1, 0), ("ar0", 0, 0, 1), ("ar0", 1, 1, 1)],
-    ("b", 37): [("dq2", 1, 1, 4), ("dq1", 0, 0, 1), ("dq1", 1, 1, 1)],
-    ("b", 38): [("dq1", 0, 1, 0), ("ds0", 1, 1, 2), ("ds0", 1, 0, 2)],
-    ("b", 39): [("dq2", 0, 1, 3), ("ds0", 0, 0, 2), ("ds0", 0, 1, 2), ("ar1", 1, 0, 2)],
-    ("b", 40): [("dq2", 1, 0, 3), ("ar1", 1, 1, 3), ("ar1", 0, 1, 2)],
-    ("b", 41): [("dq1", 1, 0, 0), ("ar1", 0, 0, 3)],
-    ("b", 42): [("dq2", 0, 0, 3), ("ar0", 1, 1, 0)],
-    ("b", 43): [("dq2", 1, 1, 3), ("ar0", 0, 0, 0), ("as0", "start")],
-    ("b", 44): [("dq1", 0, 0, 0), ("dq1", 1, 1, 0), ("ds1", "start"), ("ds0", 1, 1, 3)],
-    ("b", 45): [("dq2", 0, 1, 2), ("ds0", 1, 0, 3), ("ds0", 0, 0, 3), ("ar1", 1, 0, 1), ("ds0", 0, 1, 3)],
-    ("b", 46): [("dq2", 1, 0, 2), ("ar1", 0, 1, 1)],
-    ("b", 47): [("dq2", 0, 0, 2), ("dq2", 1, 1, 2), ("ar2", 0, 1, 3), ("ar2", 1, 0, 3), ("ar2", 0, 0, 4), ("ar2", 1, 1, 4), ("ar1", 0, 0, 2), ("ar1", 1, 1, 2)],
+    ("b", 20): [("att", 0, 0, 2)],
+    ("b", 21): [("dq0", 0, 1, 2), ("att", 1, 1, 2)],
+    ("b", 22): [("dq0", 1, 0, 2), ("dq0", 0, 0, 2)],
+    ("b", 23): [("dq0", 1, 1, 2), ("att", 1, 0, 2), ("att", 0, 1, 2), ("ar0", 0, 1, 3), ("ar0", 1, 0, 3), ("ar0", 0, 0, 4), ("ar0", 1, 1, 4)],
+    ("b", 24): [("dq0", 0, 1, 1)],
+    ("b", 25): [("dq0", 1, 0, 1), ("dq0", 0, 0, 1)],
+    ("b", 26): [("dq0", 1, 1, 1), ("dq1", 0, 0, 4)],
+    ("b", 27): [("dq1", 1, 1, 4)],
+    ("b", 28): [("att", 0, 1, 3), ("ar0", 0, 1, 2)],
+    ("b", 29): [("dq1", 0, 1, 3), ("att", 1, 1, 3), ("att", 1, 0, 3), ("ar0", 0, 0, 3), ("ar0", 1, 0, 2), ("dq0", 0, 1, 0), ("ar0", 1, 1, 3)],
+    ("b", 30): [("dq0", 1, 0, 0), ("dq0", 0, 0, 0), ("dq1", 1, 0, 3)],
+    ("b", 31): [("dq0", 1, 1, 0), ("ds0", "start"), ("dq1", 0, 0, 3)],
+    ("b", 32): [("dq1", 1, 1, 3), ("ar0", 0, 1, 1)],
+    ("b", 33): [("dq1", 0, 1, 2)],
+    ("b", 34): [("ar0", 0, 0, 2), ("ar0", 1, 0, 1), ("ds0", 0, 0, 1)],
+    ("b", 35): [("dq1", 0, 0, 2), ("dq1", 1, 0, 2), ("att", 1, 1, 4), ("ar1", 0, 1, 3), ("ar1", 1, 0, 3), ("ar1", 0, 0, 4), ("ar1", 1, 1, 4), ("ar0", 1, 1, 2), ("ds0", 0, 1, 1)],
+    ("b", 36): [("ar0", 0, 1, 0), ("ds0", 1, 1, 1), ("ds0", 1, 0, 1)],
+    ("b", 37): [("dq1", 0, 1, 1), ("dq1", 1, 1, 2), ("ar0", 0, 0, 1)],
+    ("b", 38): [("dq2", 0, 0, 4), ("ar0", 1, 0, 0), ("ds0", 0, 0, 2)],
+    ("b", 39): [("dq1", 0, 0, 1), ("dq1", 1, 0, 1), ("dq2", 1, 1, 4), ("ar1", 0, 1, 2), ("ar1", 1, 0, 2)],
+    ("b", 40): [("ar1", 0, 0, 3), ("ar1", 1, 1, 3)],
+    ("b", 41): [("dq2", 0, 1, 3), ("ar0", 1, 1, 1), ("ds0", 0, 1, 2), ("ds0", 1, 1, 2)],
+    ("b", 42): [("dq1", 0, 1, 0), ("dq2", 1, 0, 3), ("ar0", 0, 0, 0), ("ds0", 1, 0, 2)],
+    ("b", 43): [("dq1", 1, 1, 1), ("dq2", 0, 0, 3)],
+    ("b", 44): [("dq1", 1, 0, 0), ("ds0", 0, 0, 3)],
+    ("b", 45): [("dq1", 0, 0, 0), ("dq2", 1, 1, 3)],
+    ("b", 46): [("att", 0, 0, 3), ("ar1", 0, 1, 1), ("ar1", 1, 0, 1), ("ar1", 0, 0, 2), ("ar1", 1, 1, 2)],
+    ("b", 47): [("dq2", 0, 1, 2), ("ar2", 0, 1, 3), ("ar2", 1, 0, 3), ("ar2", 0, 0, 4), ("ar2", 1, 1, 4), ("ar0", 1, 1, 0), ("as0", "start"), ("ds0", 1, 1, 3), ("dq2", 1, 0, 2), ("ds0", 0, 1, 3)],
     ("b", 5): [("dh", 0, 0, 2), ("dh", 1, 1, 2)],
     ("b", 6): [("dh", 0, 1, 2), ("dh", 1, 0, 2), ("st", 0, 0, 2), ("st", 1, 1, 2)],
     ("b", 7): [("st", 0, 1, 2), ("st", 1, 0, 2)],
     ("b", 9): [("dh", 0, 0, 3), ("dh", 1, 1, 3)],
-    ("f", 1): [("ar2", 0, 1, 2), ("ar2", 1, 0, 2), ("ar2", 0, 0, 3), ("ar2", 1, 1, 3)],
-    ("f", 10): [("dq2", 0, 0, 0), ("dq2", 1, 1, 0), ("ds2", "start")],
-    ("f", 12): [("ar2", 0, 1, 1), ("ar2", 1, 0, 1)],
-    ("f", 14): [("ar2", 0, 0, 2), ("ar2", 1, 1, 2)],
-    ("f", 17): [("ds1", 0, 0, 3), ("ds1", 1, 1, 3), ("ar1", 0, 0, 0), ("ar1", 1, 1, 0), ("as1", "start"), ("as0", 0, 0, 3), ("as0", 1, 1, 3), ("as0", 0, 1, 3), ("as0", 1, 0, 3)],
-    ("f", 19): [("ds1", 0, 1, 3), ("ds1", 1, 0, 3), ("ds2", 0, 0, 1), ("ds2", 1, 1, 1)],
-    ("f", 21): [("ds2", 0, 1, 1), ("ds2", 1, 0, 1)],
-    ("f", 23): [("ar2", 0, 1, 0), ("ar2", 1, 0, 0)],
-    ("f", 25): [("ar2", 0, 0, 1), ("ar2", 1, 1, 1)],
-    ("f", 26): [("ds1", 0, 0, 4), ("ds1", 1, 1, 4), ("as1", 0, 0, 1), ("as1", 1, 1, 1), ("as1", 0, 1, 1), ("as1", 1, 0, 1)],
-    ("f", 28): [("as0", 0, 0, 4), ("as0", 1, 1, 4)],
-    ("f", 3): [("ar1", 0, 0, 1), ("ar1", 1, 1, 1)],
-    ("f", 30): [("ds2", 0, 0, 2), ("ds2", 1, 1, 2)],
-    ("f", 32): [("ds2", 0, 1, 2), ("ds2", 1, 0, 2)],
-    ("f", 34): [("ar2", 0, 0, 0), ("ar2", 1, 1, 0), ("as2", "start")],
-    ("f", 35): [("ds2", 0, 0, 3), ("ds2", 1, 1, 3), ("ds2", 0, 1, 3), ("ds2", 1, 0, 3), ("as1", 0, 0, 2), ("as1", 1, 1, 2), ("as1", 0, 1, 2), ("as1", 1, 0, 2)],
-    ("f", 5): [("as0", 0, 0, 2), ("as0", 1, 1, 2)],
-    ("f", 7): [("as0", 0, 1, 2), ("as0", 1, 0, 2)],
-    ("f", 8): [("dq2", 0, 1, 0), ("dq2", 1, 0, 0), ("ds1", 0, 0, 2), ("ds1", 1, 1, 2), ("ds1", 0, 1, 2), ("ds1", 1, 0, 2)],
-    ("h", 0): [("as0", 0, 0, 1), ("as0", 1, 1, 1)],
-    ("h", 1): [("as0", 0, 1, 1), ("as0", 1, 0, 1)],
-    ("h", 2): [("ds1", 0, 0, 1), ("ds1", 1, 1, 1), ("ds1", 0, 1, 1), ("ds1", 1, 0, 1)],
-    ("h", 3): [("ds0", 1, 1, 4)],
-    ("h", 4): [("dq2", 0, 1, 1), ("ar1", 1, 0, 0), ("ds0", 0, 0, 4)],
-    ("h", 6): [("dq2", 1, 0, 1), ("ar1", 0, 1, 0)],
-    ("h", 7): [("dq2", 0, 0, 1), ("dq2", 1, 1, 1)],
-    ("m", 0): [("as2", 0, 0, 1), ("as2", 1, 1, 1)],
-    ("m", 1): [("as2", 0, 1, 1), ("as2", 1, 0, 1)],
-    ("m", 3): [("ds2", 0, 0, 4), ("ds2", 1, 1, 4)],
-    ("q", 0): [("as1", 0, 0, 3), ("as1", 1, 1, 3)],
-    ("q", 2): [("as1", 0, 1, 3), ("as1", 1, 0, 3)],
-    ("q", 3): [("as2", 0, 0, 2), ("as2", 1, 1, 2)],
-    ("q", 5): [("as2", 0, 1, 2), ("as2", 1, 0, 2)],
-    ("q", 7): [("as1", 0, 0, 4), ("as1", 1, 1, 4)],
-    ("q", 8): [("as2", 0, 0, 3), ("as2", 1, 1, 3), ("as2", 0, 1, 3), ("as2", 1, 0, 3), ("as2", 0, 0, 4), ("as2", 1, 1, 4)],
-    ("r", 12): [("dh", 0, 0, 4), ("dh", 1, 1, 4), ("att", "start"), ("st", 0, 0, 4), ("st", 1, 1, 4)],
+    ("f", 1): [("dq2", 1, 1, 1), ("dq2", 0, 1, 0), ("ar2", 1, 0, 1), ("ar1", 0, 0, 0)],
+    ("f", 10): [("dq2", 0, 0, 0), ("ds1", 1, 0, 2)],
+    ("f", 12): [("dq2", 1, 1, 0), ("ds2", "start"), ("ar2", 0, 1, 0)],
+    ("f", 14): [("ar2", 1, 0, 0), ("as1", 0, 0, 1)],
+    ("f", 16): [("as1", 0, 1, 1), ("as1", 1, 1, 1)],
+    ("f", 17): [("ar2", 0, 0, 1), ("ar2", 1, 1, 1), ("as1", 1, 0, 1), ("as0", 0, 0, 3), ("as0", 0, 1, 3), ("as0", 1, 1, 3)],
+    ("f", 19): [("ds1", 0, 0, 3), ("as0", 1, 0, 3)],
+    ("f", 21): [("ds1", 0, 1, 3), ("ds1", 1, 1, 3)],
+    ("f", 23): [("ds2", 0, 0, 1), ("ds1", 1, 0, 3), ("ds2", 0, 1, 1)],
+    ("f", 25): [("ds2", 1, 1, 1)],
+    ("f", 26): [("ar2", 0, 0, 0), ("ar2", 1, 1, 0), ("as2", "start"), ("as1", 0, 0, 2), ("as1", 0, 1, 2), ("as1", 1, 1, 2), ("as0", 0, 0, 4), ("as1", 1, 0, 2), ("ds2", 1, 0, 1)],
+    ("f", 28): [("ds1", 0, 0, 4)],
+    ("f", 3): [("ar2", 0, 1, 1), ("ar1", 1, 1, 0), ("as1", "start")],
+    ("f", 30): [("as0", 1, 1, 4), ("ds2", 0, 0, 2), ("ds1", 1, 1, 4)],
+    ("f", 32): [("ds2", 0, 1, 2), ("ds2", 1, 1, 2)],
+    ("f", 34): [("as2", 0, 0, 1), ("as2", 1, 1, 1)],
+    ("f", 35): [("as2", 0, 1, 1), ("as2", 1, 0, 1), ("as1", 0, 0, 3), ("as1", 1, 1, 3), ("as1", 0, 1, 3), ("as1", 1, 0, 3)],
+    ("f", 5): [("ar2", 1, 1, 2), ("ar2", 0, 0, 2)],
+    ("f", 7): [("as0", 1, 1, 2), ("as0", 0, 0, 2)],
+    ("f", 8): [("dq2", 1, 0, 0), ("as0", 1, 0, 2), ("as0", 0, 1, 2), ("ds1", 0, 0, 2), ("ds1", 0, 1, 2), ("ds1", 1, 1, 2)],
+    ("h", 0): [("dq1", 1, 1, 0), ("ds1", "start"), ("dq2", 0, 0, 2), ("dq2", 1, 1, 2), ("dq2", 0, 1, 1), ("ar2", 1, 0, 2), ("ar1", 0, 1, 0), ("ar1", 1, 0, 0), ("ar1", 0, 0, 1), ("ar1", 1, 1, 1), ("ds0", 1, 0, 3), ("ds0", 0, 0, 4)],
+    ("h", 1): [("ar2", 0, 1, 2), ("ar2", 1, 1, 3)],
+    ("h", 2): [("ar2", 0, 0, 3), ("as0", 1, 1, 1)],
+    ("h", 3): [("as0", 0, 0, 1), ("as0", 1, 0, 1)],
+    ("h", 4): [("as0", 0, 1, 1), ("ds0", 1, 1, 4)],
+    ("h", 5): [("dq2", 1, 0, 1), ("ds1", 0, 0, 1), ("ds1", 0, 1, 1)],
+    ("h", 6): [("ds1", 1, 1, 1), ("ds1", 1, 0, 1)],
+    ("h", 7): [("dq2", 0, 0, 1)],
+    ("m", 0): [("ds2", 0, 0, 3), ("ds2", 1, 0, 2)],
+    ("m", 1): [("ds2", 0, 1, 3), ("ds2", 1, 1, 3)],
+    ("m", 2): [("as2", 0, 0, 2), ("as2", 1, 1, 2)],
+    ("m", 3): [("as2", 0, 1, 2), ("as2", 1, 0, 2)],
+    ("m", 4): [("ds2", 0, 0, 4), ("ds2", 1, 0, 3), ("ds2", 1, 1, 4)],
+    ("p", 3): [("att", 0, 0, 4)],
+    ("q", 0): [("as1", 0, 0, 4), ("as1", 1, 1, 4), ("as2", 0, 0, 3)],
+    ("q", 1): [("as2", 1, 1, 3)],
+    ("q", 2): [("as2", 0, 1, 3)],
+    ("q", 3): [("as2", 1, 0, 3)],
+    ("q", 6): [("as2", 0, 0, 4)],
+    ("q", 7): [("as2", 1, 1, 4)],
 }
 
 
@@ -1112,7 +1114,7 @@
             k_c, v_c, kt_c, qz, wo2, wq2, wk2, wv2, memory, mem_p, y_all, go_all, w_gate, w_up, w_down)
         cube = (dim, heads, hd)
         g_wk, g_wv = (g.reshape(inner, dim) for g in (g_wk, g_wv))
-        g_mem, g_wq, g_wk, g_wv, g_wo, g_down, g_gate, g_up = finish_call(g_mem, g_wq, g_wk, g_wv, g_wo, g_down, g_gate, g_up)
+        g_dec, g_mem, g_wq, g_wk, g_wv, g_wo, g_down, g_gate, g_up = finish_call(g_dec, g_mem, g_wq, g_wk, g_wv, g_wo, g_down, g_gate, g_up)
         g_wq, g_wk, g_wv = (g.T.reshape(cube) for g in (g_wq, g_wk, g_wv))
         return (g_dec, g_mem, gvec[0], g_wq, g_wk, g_wv, g_wo.reshape(heads, hd, dim), gvec[1], g_gate, g_up, g_down)
 

time: 275 us -> 274 us (level)
  no operation moved by 1% of the time
where the time goes in v4:
time: 274 us
  Pallas kernels  265 us (97%)
  local copies, waits for them, and re-layouts  6.75 us (2%)
    pallas_call x1, Pallas kernels, bwd_call(): pl.pallas_call(functools.partial(bwd_kernel, dims), out_shape=(S((2, dim)...  156 us
    pallas_call x1, Pallas kernels, fwd_call(): pl.pallas_call(functools.partial(fwd_kernel, dims), out_shape=(S((inner +...  87.8 us
    pallas_call x1, Pallas kernels, finish_call(): pl.pallas_call(functools.partial(finish_kernel, slots), out_shape=tuple((...  21.7 us

profile of v4, /device:TPU:21, one launch (start us, length us, event | category | flops | bytes accessed | tf_op | source)
XLA Modules:
  0.0 273.7 jit_solution(7275156811580842771)
XLA Ops:
  0.6 0.0 copy-start
  1.4 0.0 copy-start.1
  1.4 2.5 copy.27.wq_hbm
  3.9 0.0 copy-done
  3.9 1.4 copy.28.wk_hbm
  5.3 0.0 copy-done.1
  5.3 1.4 copy.29.wv_hbm
  6.8 87.8 %attn_fwd.1 = (f32[392,256]{1,0:T(8,128)}, bf16[128,768]{1,0:T(8,128)(2,1)}, bf16[128,768]{1,0:T(8,128)(2,1)}, f32[128,768]{1,0:T(8,128)}, f32[8,256]{1,0:T(8,12...) custom-call(s32[1]{0:T(128)S(6)} %copy.33.len_ref, ...), custom_call_target="tpu_custom_call" | custom-call | flops 10000000000 | bytes 31457280 | tf_op jit(solution)/shard_map/attn_fwd/pallas_call | solution.py:1074
  94.6 156.0 %attn_bwd.1 = (f32[2,768]{1,0:T(2,128)}, f32[128,768]{1,0:T(8,128)}, f32[1024,768]{1,0:T(8,128)}, f32[2,3,4,2,16,768]{5,4,3,2,1,0:T(8,128)}, f32[2,3,4,2,16,768]...) custom-call(s32[1]{0:T(128)S(6)} %copy.33.len_ref, ...), custom_call_target="tpu_custom_call" | custom-call | flops 10000000000 | bytes 31457280 | tf_op jit(solution)/shard_map/attn_bwd/pallas_call | solution.py:770
  250.6 21.7 %finish.1 = (f32[128,768]{1,0:T(8,128)}, f32[1024,768]{1,0:T(8,128)}, f32[768,768]{1,0:T(8,128)}, f32[768,768]{1,0:T(8,128)}, f32[768,768]{1,0:T(8,128)}, /*inde...) custom-call(f32[128,768]{1,0:T(8,128)} %get-tuple-element.54.refs_0_, ...), custom_call_target="tpu_custom_call" | custom-call | tf_op jit(solution)/shard_map/finish/pallas_call | solution.py:821
  272.3 1.4 slice_reduce_fusion
Async XLA Ops:
  0.6 3.2 %copy-start = (bf16[768,12,64]{0,2,1:T(8,128)(2,1)S(1)}, bf16[768,12,64]{0,2,1:T(8,128)(2,1)}, u32[]{:S(2)}) copy-start(bf16[768,12,64]{0,2,1:T(8,128)(2,1)} %param.19) | copy-start | bytes 3538948
  1.4 3.9 %copy-start.1 = (bf16[768,12,64]{0,2,1:T(8,128)(2,1)S(1)}, bf16[768,12,64]{0,2,1:T(8,128)(2,1)}, u32[]{:S(2)}) copy-start(bf16[768,12,64]{0,2,1:T(8,128)(2,1)} %param.20) | copy-start | bytes 3538948
